TPU v7x, 256 devices: a whole 4x4x8 slice. The times are simulated.
256 devices in a mesh: space: 128 (over y, z, x), grp: 2 (over core).
Axes of the slice: x: 4, y: 4, z: 8, core: 2. Of those that a mesh axis runs over, the one named last changes fastest.
Arguments:
- echoes: bfloat16 [1280, 300, 2048], P(('space', 'grp'))
- frame_count: int32 [1280], replicated, may hold values from 0 to 300, as said below
- clutter_rank: int32 [1280], replicated, may hold values from 1 to 24
- noise_rank: int32 [1280], replicated, may hold values from 48 to 96
- start_basis: float32 [300, 96], replicated, may hold values from -6 to 6
Outputs:
- volume: float32 [300, 1310720], P(None, ('space', 'grp'))
- power: float32 [1310720], P(('space', 'grp'))
Inputs may be any that keep to these rules, and one draw needn't show every extreme that they name: `frame_count`: within each holder's 5 consecutive slots the slots with frames come first and the others have 0 frames; every holder has 1 to 5 slots with frames, some holder has all 5; two holders with the same grp index whose space indices lie half the space axis apart have at most 6 slots with frames together; a slot with frames has 150 or more.
All inputs are finite; a program needn't handle non-finite values.
Results may differ from a plain program's by a relative error of at most 0.0056.
Values may be sent and summed in bfloat16 or wider, within the bound.
A program may use at most 128 MiB of HBM per device.

v0:
```python
import functools

import jax
import jax.numpy as jnp
from jax import lax
from jax.sharding import Mesh
from jax.sharding import PartitionSpec as P

ITERS = 4
OWN = 3
SPACE = ("space_0", "space_1", "space_2")
SPACE_GRP = ("space_0", "space_1", "space_2", "grp")


def swapped(block, axis, stride):
    count = lax.axis_size(axis)
    route = []
    for low in range(count):
        high = low | 1 << stride
        if high != low and high < count:
            route += [(low, high), (high, low)]
    return lax.ppermute(block, axis, route)


def passed_along(value, axis, steps):
    count = lax.axis_size(axis)
    initial, last = (max(0, -steps), min(count, count - steps))
    return lax.ppermute(value, axis, [(source, source + steps) for source in range(initial, last)])


def one_axis_at_a_time(shard, axes):
    return functools.reduce(lax.psum, axes, shard)


def filter_block(echo_block, frame_total, clutter_cut, noise_cut, initial):
    frames = jnp.arange(echo_block.shape[0], dtype=jnp.int32)
    frame_mask = (frames < frame_total).astype(jnp.bfloat16)
    padding_diag = (frames >= frame_total).astype(jnp.float32)
    masked = echo_block * frame_mask[:, None]
    gram_matrix = jnp.dot(masked, masked.T, preferred_element_type=jnp.float32) + jnp.diag(
        padding_diag
    )
    subspace = initial
    for iteration in range(ITERS):
        product = jnp.dot(gram_matrix, subspace, precision=lax.Precision.HIGHEST)
        inner_gram = jnp.dot(product.T, product, precision=lax.Precision.HIGHEST)
        factor = jnp.linalg.cholesky(inner_gram)
        subspace = jax.scipy.linalg.solve_triangular(factor, product.T, lower=True).T
    basis = subspace.astype(jnp.bfloat16)
    coefficients = jnp.dot(basis.T, masked, preferred_element_type=jnp.float32)
    columns = jnp.arange(basis.shape[1], dtype=jnp.int32)
    band_mask = ((columns >= clutter_cut) & (columns < noise_cut)).astype(jnp.float32)
    coefficients = (coefficients * band_mask[:, None]).astype(jnp.bfloat16)
    return jnp.dot(basis, coefficients, preferred_element_type=jnp.float32).astype(jnp.bfloat16)


def block_ints(device, hold, frame_count, clutter_rank, noise_rank):
    first_block = device * hold
    return tuple(
        (
            lax.dynamic_slice_in_dim(source, first_block, hold)
            for source in (frame_count, clutter_rank, noise_rank)
        )
    )


def shards(echoes, frame_count, clutter_rank, noise_rank, start_basis):
    space_count = lax.axis_size(SPACE)
    pair_count = lax.axis_size("grp")
    hold = echoes.shape[0]
    space_index = lax.axis_index(SPACE)
    grp_index = lax.axis_index("grp")
    device = space_index * pair_count + grp_index
    frames_home, clutter_home, noise_home = block_ints(
        device, hold, frame_count, clutter_rank, noise_rank
    )
    runner = jax.vmap(filter_block, in_axes=(0, 0, 0, 0, None))
    partner = (space_index + space_count // 2) % space_count * pair_count + grp_index
    far_ints = block_ints(partner, hold, frame_count, clutter_rank, noise_rank)
    far_frames, far_clutter, far_noise = [piece[OWN:][::-1] for piece in far_ints]
    far_live = far_frames > 0
    bit_number = space_count.bit_length() - 2
    low_slot = OWN - (hold - OWN)
    incoming = swapped(echoes[OWN:], SPACE, bit_number)
    mixed_echo = jnp.where(far_live[:, None, None], incoming[::-1], echoes[low_slot:OWN])
    work_echo = jnp.concatenate([echoes[:low_slot], mixed_echo], axis=0)
    work_frames = jnp.concatenate(
        [frames_home[:low_slot], jnp.where(far_live, far_frames, frames_home[low_slot:OWN])]
    )
    work_clutter = jnp.concatenate(
        [clutter_home[:low_slot], jnp.where(far_live, far_clutter, clutter_home[low_slot:OWN])]
    )
    work_noise = jnp.concatenate(
        [noise_home[:low_slot], jnp.where(far_live, far_noise, noise_home[low_slot:OWN])]
    )
    cleaned = runner(work_echo, work_frames, work_clutter, work_noise, start_basis)
    returned = swapped(cleaned[low_slot:][::-1], SPACE, bit_number)
    empty_blocks = jnp.zeros_like(returned)
    home_live = frames_home[OWN:] > 0
    tail_part = jnp.where(home_live[:, None, None], returned, empty_blocks)
    middle_part = jnp.where(far_live[:, None, None], empty_blocks, cleaned[low_slot:])
    cleaned_home = jnp.concatenate([cleaned[:low_slot], middle_part, tail_part], axis=0)
    width = cleaned_home.shape[2]
    half_width = width // 2
    window = jnp.sin(jnp.pi * (jnp.arange(width, dtype=jnp.float32) + 0.5) / width) ** 2
    weighted = cleaned_home.astype(jnp.float32) * window
    border = passed_along(weighted[0, :, :half_width], SPACE_GRP, -1)
    following = jnp.concatenate([weighted[1:, :, :half_width], border[None]], axis=0)
    regions = weighted[:, :, half_width:] + following
    frames_total = regions.shape[1]
    volume = jnp.transpose(regions, (1, 0, 2)).reshape(frames_total, -1)
    strength = jnp.sum(volume * volume, axis=0) / frames_total
    total = one_axis_at_a_time(jnp.sum(strength), SPACE_GRP)
    mean_level = total / (strength.shape[0] * space_count * pair_count)
    power = strength / (mean_level + 1e-06)
    return (volume, power)


def solution(mesh):
    finer = Mesh(
        mesh.devices.reshape(4, 8, 4, mesh.shape["grp"]), ("space_0", "space_1", "space_2", "grp")
    )
    in_specs = (P(SPACE_GRP, None, None), P(), P(), P(), P())
    out_specs = (P(None, SPACE_GRP), P(SPACE_GRP))
    return jax.shard_map(
        shards, mesh=finer, in_specs=in_specs, out_specs=out_specs, check_vma=False
    )
```

profile of v0, /device:TPU:1, one launch (start us, length us, event | category | flops | bytes accessed | tf_op | source)
XLA Modules:
  0.0 437.9 jit_solution(11111294689932616343)
XLA Ops:
  0.7 1.8 slice-done
  2.4 4.0 copy.51
  6.4 3.7 collective-permute-start
  10.1 2.5 slice.63
  16.1 46.4 %collective-permute-done = bf16[2,300,2048]{2,0,1:T(2,128)(2,1)S(1)} collective-permute-done((bf16[2,300,2048]{2,0,1:T(2,128)(2,1)}, bf16[2,300,2048]{2,0,1:T(2,128)(2,1)S(1)}, u32[]{:S(2)}, u32[]{:S(2)}) %collective-permute-start) | collective-permute-done | bytes 2457632 | tf_op jit(solution)/shard_map/ppermute | solution.py:22
  63.5 3.0 slice_select_fusion
  66.6 2.2 fusion.5
  68.9 1.7 fusion.22
  71.3 26.6 %custom-call.12 = f32[3,96,96]{2,1,0:T(8,128)S(1)} custom-call(f32[3,96,96]{2,1,0:T(8,128)S(1)} %fusion.21), custom_call_target="Cholesky" | custom-call | tf_op jit(solution)/shard_map/vmap(jit(cholesky))/cholesky | solution.py:47
  98.1 22.1 %custom-call.13 = f32[3,1,96,96]{2,3,1,0:T(8,128)S(1)} custom-call(f32[3,1,96,96]{3,2,1,0:T(8,128)S(1)} %select_bitcast_fusion.3), custom_call_target="InvertDiagBlocksLowerTriangular" | custom-call | tf_op jit(solution)/shard_map/vmap(jit(_solve_triangular))/triangular_solve | solution.py:48
  123.3 26.4 %custom-call.14 = f32[3,96,96]{2,1,0:T(8,128)S(1)} custom-call(f32[3,96,96]{2,1,0:T(8,128)S(1)} %fusion.19), custom_call_target="Cholesky" | custom-call | tf_op jit(solution)/shard_map/vmap(jit(cholesky))/cholesky | solution.py:47
  149.9 22.4 %custom-call.15 = f32[3,1,96,96]{2,3,1,0:T(8,128)S(1)} custom-call(f32[3,1,96,96]{3,2,1,0:T(8,128)S(1)} %select_bitcast_fusion.2), custom_call_target="InvertDiagBlocksLowerTriangular" | custom-call | tf_op jit(solution)/shard_map/vmap(jit(_solve_triangular))/triangular_solve | solution.py:48
  175.3 26.4 %custom-call.16 = f32[3,96,96]{2,1,0:T(8,128)S(1)} custom-call(f32[3,96,96]{2,1,0:T(8,128)S(1)} %fusion.17), custom_call_target="Cholesky" | custom-call | tf_op jit(solution)/shard_map/vmap(jit(cholesky))/cholesky | solution.py:47
  201.9 22.1 %custom-call.17 = f32[3,1,96,96]{2,3,1,0:T(8,128)S(1)} custom-call(f32[3,1,96,96]{3,2,1,0:T(8,128)S(1)} %select_bitcast_fusion.1), custom_call_target="InvertDiagBlocksLowerTriangular" | custom-call | tf_op jit(solution)/shard_map/vmap(jit(_solve_triangular))/triangular_solve | solution.py:48
  227.1 26.4 %custom-call.18 = f32[3,96,96]{2,1,0:T(8,128)S(1)} custom-call(f32[3,96,96]{2,1,0:T(8,128)S(1)} %fusion.15), custom_call_target="Cholesky" | custom-call | tf_op jit(solution)/shard_map/vmap(jit(cholesky))/cholesky | solution.py:47
  253.7 22.4 %custom-call.19 = f32[3,1,96,96]{2,3,1,0:T(8,128)S(1)} custom-call(f32[3,1,96,96]{3,2,1,0:T(8,128)S(1)} %select_bitcast_fusion), custom_call_target="InvertDiagBlocksLowerTriangular" | custom-call | tf_op jit(solution)/shard_map/vmap(jit(_solve_triangular))/triangular_solve | solution.py:48
  276.8 5.6 %convolution_convert_fusion = bf16[3,300,2048]{2,1,0:T(8,128)(2,1)} fusion(bf16[3,96,300]{2,1,0:T(8,128)(2,1)S(1)} %convolution_convert_fusion.1, bf16[2,300,2048]{2,1,0:T(8,128)(2,1)} %copy-done.3, bf16[1,300,2048]{2,1,0:T(8,128)(2,1)S(1)} %copy-done.4, bf16[3,300]{1,0:T(4,128)(2,1)S(1)} %copy-done.6, f32[3,96]{1,0:T(4,128)S(1)} %copy-done.7), kind=kOutput, calls=%fused_computation.5 | convolution fusion | flops 714498048 | bytes 7548552 | tf_op jit(solution)/shard_map/vmap()/dot_general | solution.py:54
  282.4 4.2 broadcast_select_fusion
  286.6 1.9 rev.19
  288.5 2.5 copy.43
  291.1 3.7 collective-permute-start.1
  294.9 51.8 %collective-permute-done.1 = bf16[2,300,2048]{2,0,1:T(2,128)(2,1)S(1)} collective-permute-done((bf16[2,300,2048]{2,0,1:T(2,128)(2,1)S(1)}, bf16[2,300,2048]{2,0,1:T(2,128)(2,1)S(1)}, u32[]{:S(2)}, u32[]{:S(2)}) %collective-permute-start.1) | collective-permute-done | bytes 2457632 | tf_op jit(solution)/shard_map/ppermute | solution.py:22
  348.3 2.4 convert_multiply_fusion
  350.8 4.3 collective-permute-start.2
  355.9 14.9 %collective-permute-done.2 = f32[300,1024]{1,0:T(8,128)S(1)} collective-permute-done((f32[300,1024]{1,0:T(8,128)S(1)}, f32[300,1024]{1,0:T(8,128)S(1)}, u32[]{:S(2)}, u32[]{:S(2)}) %collective-permute-start.2) | collective-permute-done | bytes 1228832 | tf_op jit(solution)/shard_map/ppermute | solution.py:28
  370.8 3.5 multiply_reduce_fusion
  374.9 9.3 %psum.28 = f32[]{:T(128)} all-reduce(f32[]{:T(128)} %multiply_reduce_fusion.1), channel_id=1, replica_groups=mesh['space_0'=4,'space_1'=8,'space_2'=4,'grp'=2] {'space_0'}, use_global_device_ids=true, to_apply=%region_4.7 | all-reduce | flops 1 | bytes 8 | tf_op jit(solution)/shard_map/psum | solution.py:32
  384.2 16.9 %psum.29 = f32[]{:T(128)} all-reduce(f32[]{:T(128)} %psum.28), channel_id=1, replica_groups=mesh['space_0'=4,'space_1'=8,'space_2'=4,'grp'=2] {'space_1'}, use_global_device_ids=true, to_apply=%region_5.8 | all-reduce | flops 1 | bytes 8 | tf_op jit(solution)/shard_map/psum | solution.py:32
  401.0 10.1 %psum.30 = f32[]{:T(128)} all-reduce(f32[]{:T(128)} %psum.29), channel_id=1, replica_groups=mesh['space_0'=4,'space_1'=8,'space_2'=4,'grp'=2] {'space_2'}, use_global_device_ids=true, to_apply=%region_6.9 | all-reduce | flops 1 | bytes 8 | tf_op jit(solution)/shard_map/psum | solution.py:32
  411.2 8.3 %psum.31 = f32[]{:T(128)} all-reduce(f32[]{:T(128)} %psum.30), channel_id=1, replica_groups=mesh['space_0'=4,'space_1'=8,'space_2'=4,'grp'=2] {'grp'}, use_global_device_ids=true, to_apply=%region_7.10 | all-reduce | flops 1 | bytes 8 | tf_op jit(solution)/shard_map/psum | solution.py:32
  420.7 8.3 %copy.45 = f32[300,5,1024]{0,2,1:T(8,128)} copy(f32[300,5,1024]{2,0,1:T(8,128)} %get-tuple-element.11) | data formatting | bytes 12288000 | tf_op jit(solution)/shard_map/transpose | solution.py:111
  429.0 8.5 %copy.46 = f32[300,5120]{1,0:T(8,128)} copy(f32[300,5120]{0,1:T(8,128)} %bitcast.78) | data formatting | bytes 12288000
  (85 shorter events, 19.6 us)
Async XLA Ops:
  0.6 68.2 %copy-start = (f32[300,96]{0,1:T(8,128)S(1)}, f32[300,96]{0,1:T(8,128)}, u32[]{:S(2)}) copy-start(f32[300,96]{0,1:T(8,128)} %param.12) | copy-start | bytes 345604
  0.6 1.8 slice-start
  6.4 56.1 %collective-permute-start = (bf16[2,300,2048]{2,0,1:T(2,128)(2,1)}, bf16[2,300,2048]{2,0,1:T(2,128)(2,1)S(1)}, u32[]{:S(2)}, u32[]{:S(2)}) collective-permute-start(bf16[2,300,2048]{2,0,1:T(2,128)(2,1)} %copy.51), channel_id=1, source_target_pairs={{0,128},{128,0},{2,130},{130,2},{4,132},{132,4},{6,134},{134,6},{8... | collective-permute-start | bytes 7372808 | tf_op jit(solution)/shard_map/ppermute | solution.py:22
  13.5 49.0 %copy-start.8 = (s32[5]{0:T(128)}, s32[5]{0:T(128)S(1)}, u32[]{:S(2)}) copy-start(s32[5]{0:T(128)S(1)} %get-tuple-element.18) | copy-start | bytes 64
  15.3 51.2 %copy-start.10 = (pred[2]{0:T(512)(128)(4,1)}, pred[2]{0:T(512)(128)(4,1)S(1)}, u32[]{:S(2)}) copy-start(pred[2]{0:T(512)(128)(4,1)S(1)} %broadcast_compare_fusion) | copy-start | bytes 10
  16.1 50.5 %copy-start.5 = (bf16[3,300]{1,0:T(4,128)(2,1)}, bf16[3,300]{1,0:T(4,128)(2,1)S(1)}, u32[]{:S(2)}) copy-start(bf16[3,300]{1,0:T(4,128)(2,1)S(1)} %get-tuple-element.24) | copy-start | bytes 5404
  63.5 3.0 copy-start.4
  66.5 2.3 copy-start.3
  224.7 52.1 %copy-start.6 = (bf16[3,300]{1,0:T(4,128)(2,1)S(1)}, bf16[3,300]{1,0:T(4,128)(2,1)}, u32[]{:S(2)}) copy-start(bf16[3,300]{1,0:T(4,128)(2,1)} %copy-done.5) | copy-start | bytes 5404
  224.7 52.1 %copy-start.7 = (f32[3,96]{1,0:T(4,128)S(1)}, f32[3,96]{1,0:T(4,128)}, u32[]{:S(2)}) copy-start(f32[3,96]{1,0:T(4,128)} %fusion.27) | copy-start | bytes 3460
  276.7 5.7 %copy-start.11 = (pred[2]{0:T(512)(128)(4,1)S(1)}, pred[2]{0:T(512)(128)(4,1)}, u32[]{:S(2)}) copy-start(pred[2]{0:T(512)(128)(4,1)} %copy-done.10) | copy-start | bytes 10
  288.5 6.3 %copy-start.9 = (s32[5]{0:T(128)S(1)}, s32[5]{0:T(128)}, u32[]{:S(2)}) copy-start(s32[5]{0:T(128)} %copy-done.8) | copy-start | bytes 64
  291.1 55.6 %collective-permute-start.1 = (bf16[2,300,2048]{2,0,1:T(2,128)(2,1)S(1)}, bf16[2,300,2048]{2,0,1:T(2,128)(2,1)S(1)}, u32[]{:S(2)}, u32[]{:S(2)}) collective-permute-start(bf16[2,300,2048]{2,0,1:T(2,128)(2,1)S(1)} %copy.43), channel_id=1, source_target_pairs={{0,128},{128,0},{2,130},{130,2},{4,132},{132,4},{6,134},{134,6},{8... | collective-permute-start | bytes 7372808 | tf_op jit(solution)/shard_map/ppermute | solution.py:22
  294.9 53.4 %copy-start.2 = (bf16[2,300,2048]{2,1,0:T(8,128)(2,1)S(1)}, bf16[2,300,2048]{2,1,0:T(8,128)(2,1)}, u32[]{:S(2)}) copy-start(bf16[2,300,2048]{2,1,0:T(8,128)(2,1)} %get-tuple-element.12) | copy-start | bytes 7372804
  294.9 53.4 %slice-start.1 = ((bf16[3,300,2048]{2,1,0:T(8,128)(2,1)}), bf16[1,300,2048]{2,1,0:T(8,128)(2,1)S(1)}, s32[]{:S(2)}) async-start(bf16[3,300,2048]{2,1,0:T(8,128)(2,1)} %convolution_convert_fusion), calls=%async_computation.1 | async-start | bytes 2490368 | tf_op jit(solution)/shard_map/slice | solution.py:102
  350.8 20.0 %collective-permute-start.2 = (f32[300,1024]{1,0:T(8,128)S(1)}, f32[300,1024]{1,0:T(8,128)S(1)}, u32[]{:S(2)}, u32[]{:S(2)}) collective-permute-start(f32[300,1024]{1,0:T(8,128)S(1)} %slice_bitcast_fusion), channel_id=1, source_target_pairs={{1,0},{2,1},{3,2},{4,3},{5,4},{6,5},{7,6},{8,7},{9,8},{10,9},{11,1... | collective-permute-start | bytes 3686408 | tf_op jit(solution)/shard_map/ppermute | solution.py:28
  429.0 8.5 %copy-start.1 = (f32[300,96]{0,1:T(8,128)S(1)}, f32[300,96]{0,1:T(8,128)}, u32[]{:S(2)}) copy-start(f32[300,96]{0,1:T(8,128)} %param.12) | copy-start | bytes 345604
where the time goes:
time: 446 us; the launch traced here: 438 us
  other arithmetic  212 us (48%)
  waiting for transfers between devices  113 us (25%)
  blocking collectives  44.6 us (10%)
  local copies, waits for them, and re-layouts  34.7 us (8%)
  matrix products  19.3 us (4%)
  starting transfers between devices  11.7 us (3%)
    another operation x13, other arithmetic, filter_block(): factor = jnp.linalg.cholesky(inner_gram)  106 us
    ppermute x2, waiting for transfers between devices, swapped(): return lax.ppermute(block, axis, route)  98.2 us
    another operation x9, other arithmetic, filter_block(): jax.scipy.linalg.solve_triangular(factor, product.T, lower=True)  89.4 us
    psum x4, blocking collectives, one_axis_at_a_time(): return functools.reduce(lax.psum, axes, shard)  44.6 us
    ppermute x1, waiting for transfers between devices, passed_along(): lax.ppermute(value, axis, [(source, source + steps) for source in range(i...  14.9 us
    unnamed x26, local copies, waits for them, and re-layouts  12.5 us
  transfers between devices with their start and end apart: 3, of which 3 were waited for; matrix products, arithmetic and copies ran while one was open for 2% of the time, Pallas kernels for 0%

commit v1 on v0

v1 whole, which is shorter than its diff:
```python
import functools
import numpy as np
import jax, jax.numpy as jnp
from jax import lax
from jax.experimental import pallas as pl
from jax.experimental.pallas import tpu as pltpu
from jax.sharding import PartitionSpec as P

F32, BF = jnp.float32, jnp.bfloat16
ITERS = 4
CHUNK = 512

NT = (((1,), (1,)), ((), ()))
NN = (((1,), (0,)), ((), ()))

def mm(a, b, dims):
    return lax.dot_general(a, b, dims, preferred_element_type=F32)

def split(a):
    hi = a.astype(BF)
    return hi, (a - hi.astype(F32)).astype(BF)

def split3(a):
    hi = a.astype(BF)
    rest = a - hi.astype(F32)
    mid = rest.astype(BF)
    return hi, mid, (rest - mid.astype(F32)).astype(BF)

def eliminate(a_ref, s_ref, blocks, k, w, between):
    tiles = k // 8
    sub = lax.broadcasted_iota(jnp.int32, (8, 128), 0)
    lane = lax.broadcasted_iota(jnp.int32, (8, 128), 1)
    for p in range(k // w):
        j0 = p * w
        t0, r0 = j0 // 8, j0 % 8
        inside = (lane >= j0) & (lane < j0 + w)
        between(p)
        cols, diag = {}, {}
        for b in blocks:
            for t in range(t0, tiles):
                tile = a_ref[b, 8 * t:8 * t + 8, :]
                for q in range(w):
                    cols[b, q, t] = jnp.broadcast_to(tile[:, j0 + q:j0 + q + 1], (8, 128))
                if t == t0:
                    diag[b] = jnp.where(inside, 0.0, tile)
        facs, rows, scal = {}, {}, {}
        for q in range(w):
            r, j = r0 + q, j0 + q
            for b in blocks:
                pivot = jnp.broadcast_to(cols[b, q, t0][r:r + 1, :], (8, 128))
                inv = 1.0 / pivot
                root = lax.rsqrt(pivot)
                scal[b] = root if q == 0 else jnp.where(sub == r, root, scal[b])
                for t in range(t0, tiles):
                    f = cols[b, q, t] * inv
                    facs[b, q, t] = jnp.where(sub > r, f, 0.0) if t == t0 else f
                for q2 in range(q + 1, w):
                    m = jnp.broadcast_to(cols[b, q2, t0][r:r + 1, :], (8, 128))
                    for t in range(t0, tiles):
                        cols[b, q2, t] = cols[b, q2, t] - facs[b, q, t] * m
                row = jnp.broadcast_to(diag[b][r:r + 1, :], (8, 128))
                row = jnp.where(lane == j, 1.0, jnp.where((lane > j) & (lane < j0 + w), 0.0, row))
                rows[b, q] = row
                diag[b] = diag[b] - facs[b, q, t0] * row
        for b in blocks:
            a_ref[b, 8 * t0:8 * t0 + 8, :] = diag[b]
            s_ref[b, j0:j0 + w, :] = scal[b][r0:r0 + w, :]
            for t in range(t0 + 1, tiles):
                tile = jnp.where(inside, 0.0, a_ref[b, 8 * t:8 * t + 8, :])
                for q in range(w):
                    tile = tile - facs[b, q, t] * rows[b, q]
                a_ref[b, 8 * t:8 * t + 8, :] = tile


def subspace_kernel(n, w, count_of, echo_ref, *refs):
    (fc_ref, cr_ref, nr_ref, start_ref, st_ref, s_out_ref, border_ref, x_ref, first_ref, gh_ref, gl_ref, p_ref, y_ref, a_ref, s_ref) = refs
    step = pl.program_id(0)
    frames, k = start_ref.shape
    lp = gh_ref.shape[2]

    @pl.when(step == 0)
    def _():
        x_ref[...] = jnp.zeros_like(x_ref)
        gh_ref[...] = jnp.zeros_like(gh_ref)
        gl_ref[...] = jnp.zeros_like(gl_ref)
        p_ref[...] = jnp.zeros_like(p_ref)
        y_ref[...] = jnp.zeros_like(y_ref)

    total = fc_ref[count_of(step)]
    row = lax.broadcasted_iota(jnp.int32, (frames, 1), 0)
    x_ref[:frames, :] = jnp.where(row < total, echo_ref[0], jnp.zeros((), BF))
    x = x_ref[...]
    g = mm(x[:-(-frames // 16) * 16], x, NT)

    @pl.when(step == 0)
    def _():
        first_ref[...] = x_ref[:, :first_ref.shape[1]]

    gr = lax.broadcasted_iota(jnp.int32, g.shape, 0)
    gc = lax.broadcasted_iota(jnp.int32, g.shape, 1)
    g = g + jnp.where((gr == gc) & (gr >= total) & (gr < frames), 1.0, 0.0)
    hi, lo = split(g)
    gh_ref[step, :g.shape[0], :] = hi
    gl_ref[step, :g.shape[0], :] = lo

    @pl.when(step == n - 1)
    def _():
        blocks = range(n)
        s0 = start_ref[...]
        s0 = jnp.concatenate([s0, jnp.zeros((frames, 128 - k), F32)], axis=1)
        s0 = jnp.concatenate([s0, jnp.zeros((lp - frames, 128), F32)], axis=0)
        s0t = s0.T
        sh, sl = split(s0t)
        for b in blocks:
            p_ref[b, :, :] = mm(sh, gh_ref[b], NN) + mm(sh, gl_ref[b], NN) + mm(sl, gh_ref[b], NN)

        def factor(between):
            for b in blocks:
                p = p_ref[b]
                h, m, l = split3(p)
                a_ref[b, :, :] = (mm(h[:k], h, NT) + (mm(h[:k], m, NT) + mm(m[:k], h, NT))
                                  + (mm(m[:k], m, NT) + mm(h[:k], l, NT) + mm(l[:k], h, NT)))
            eliminate(a_ref, s_ref, blocks, k, w, between)

        def inverse(b):
            lower = a_ref[b]
            ri = lax.broadcasted_iota(jnp.int32, lower.shape, 0)
            ci = lax.broadcasted_iota(jnp.int32, lower.shape, 1)
            lower = jnp.where(ci < ri, lower, jnp.where(ci == ri, 1.0, 0.0))
            return lower * s_ref[b]

        def body(i, carry):
            panels = k // w
            at = {panels * (b + 1) // (n + 1): b for b in blocks}

            def between(p):
                if p in at:
                    b = at[p]
                    ph, plo = split(p_ref[b, :k, :])
                    y_ref[b, :k, :] = mm(ph, gh_ref[b], NN) + mm(ph, gl_ref[b], NN) + mm(plo, gh_ref[b], NN)
            factor(between)
            for b in blocks:
                vh, vl = split(inverse(b))
                yh, yl = split(y_ref[b])
                p_ref[b, :k, :] = mm(vh, yh, NN) + mm(vh, yl, NN) + mm(vl, yh, NN)
            return carry

        lax.fori_loop(0, ITERS - 1, body, 0)
        factor(lambda p: None)
        for b in blocks:
            vh, vl = split(inverse(b))
            ph, plo = split(p_ref[b])
            st = mm(vh, ph, NN) + mm(vh, plo, NN) + mm(vl, ph, NN)
            st = jnp.concatenate([st, jnp.zeros((128 - k, lp), F32)], axis=0)
            st_ref[b, :, :] = st.astype(BF)
            s_out_ref[b, :, :] = st.T.astype(BF)
        slot = count_of(0)
        band = band_of(k, cr_ref[slot], nr_ref[slot])
        basis = st_ref[0, :k, :]
        border_ref[:, :lp] = basis
        border_ref[:, lp:] = (mm(basis, first_ref[...], NN) * band).astype(BF)


def subspace(echoes, fc, cr, nr, start, count_of, w=4):
    n, frames, width = echoes.shape
    k = start.shape[1]
    lp = -(-frames // 128) * 128
    smem = pl.BlockSpec(memory_space=pltpu.SMEM)
    edge = (k, lp + width // 2)
    return pl.pallas_call(
        functools.partial(subspace_kernel, n, w, count_of),
        grid=(n,),
        in_specs=[pl.BlockSpec((1, frames, width), lambda i: (i, 0, 0)),
                  smem, smem, smem,
                  pl.BlockSpec((frames, k), lambda i: (0, 0))],
        out_specs=[pl.BlockSpec((n, 128, lp), lambda i: (0, 0, 0)),
                   pl.BlockSpec((n, lp, 128), lambda i: (0, 0, 0)),
                   pl.BlockSpec(edge, lambda i: (0, 0))],
        out_shape=[jax.ShapeDtypeStruct((n, 128, lp), BF), jax.ShapeDtypeStruct((n, lp, 128), BF),
                   jax.ShapeDtypeStruct(edge, BF)],
        scratch_shapes=[pltpu.VMEM((lp, width), BF), pltpu.VMEM((lp, width // 2), BF), pltpu.VMEM((n, lp, lp), BF), pltpu.VMEM((n, lp, lp), BF),
                        pltpu.VMEM((n, 128, lp), F32), pltpu.VMEM((n, 128, lp), F32),
                        pltpu.VMEM((n, k, 128), F32), pltpu.VMEM((n, k, 128), F32)],
        compiler_params=pltpu.CompilerParams(vmem_limit_bytes=60 << 20),
        name="subspace",
    )(echoes, fc, cr, nr, start)


def project_kernel(n, count_of, echo_ref, st_ref, s_ref, fc_ref, cr_ref, nr_ref, win_ref, vol_ref, str_ref, last_ref,
                   x_ref, coef_ref, prev_ref):
    step = pl.program_id(0)
    frames, width = echo_ref.shape[1:]
    half = width // 2
    k = coef_ref.shape[0] - 32
    rows = prev_ref.shape[0]

    @pl.when(step == 0)
    def _():
        x_ref[...] = jnp.zeros_like(x_ref)
        coef_ref[...] = jnp.zeros_like(coef_ref)

    slot = count_of(step)
    total = fc_ref[slot]
    fr = lax.broadcasted_iota(jnp.int32, (frames, 1), 0)
    band = band_of(k, cr_ref[slot], nr_ref[slot])
    x_ref[:frames, :] = jnp.where(fr < total, echo_ref[0], jnp.zeros((), BF))
    st, s = st_ref[0, :k, :], s_ref[0, :rows, :]
    for c in range(width // CHUNK):
        at = slice(c * CHUNK, (c + 1) * CHUNK)
        coef_ref[:k, at] = (mm(st, x_ref[:, at], NN) * band).astype(BF)

    @pl.when(step > 0)
    def _():
        for c in range(half // CHUNK):
            at = slice(c * CHUNK, (c + 1) * CHUNK)
            low = mm(s, coef_ref[:, at], NN).astype(BF).astype(F32)
            vol = (prev_ref[:, at] + low * win_ref[:, at])[:frames]
            vol_ref[:, at] = vol
            str_ref[:, at] = jnp.sum(vol * vol, axis=0, keepdims=True) / frames

    for c in range(half // CHUNK):
        at, up = slice(c * CHUNK, (c + 1) * CHUNK), slice(half + c * CHUNK, half + (c + 1) * CHUNK)
        prev_ref[:, at] = mm(s, coef_ref[:, up], NN).astype(BF).astype(F32) * win_ref[:, up]

    @pl.when(step == n - 1)
    def _():
        last_ref[...] = prev_ref[...]


def band_of(k, low, high):
    col = lax.broadcasted_iota(jnp.int32, (k, 1), 0)
    return jnp.where((col >= low) & (col < high), 1.0, 0.0)


def project(echoes, st, s, fc, cr, nr, window, count_of):
    n, frames, width = echoes.shape
    half, lp, k = width // 2, st.shape[2], st.shape[1] - 32
    rows = -(-frames // 16) * 16
    smem = pl.BlockSpec(memory_space=pltpu.SMEM)
    after = lambda i: (0, jnp.maximum(i - 1, 0))
    return pl.pallas_call(
        functools.partial(project_kernel, n, count_of),
        grid=(n,),
        in_specs=[pl.BlockSpec((1, frames, width), lambda i: (i, 0, 0)),
                  pl.BlockSpec((1, 128, lp), lambda i: (i, 0, 0)),
                  pl.BlockSpec((1, lp, 128), lambda i: (i, 0, 0)),
                  smem, smem, smem,
                  pl.BlockSpec((1, width), lambda i: (0, 0))],
        out_specs=[pl.BlockSpec((frames, half), after), pl.BlockSpec((1, half), after),
                   pl.BlockSpec((rows, half), lambda i: (0, 0))],
        out_shape=[jax.ShapeDtypeStruct((frames, n * half), F32), jax.ShapeDtypeStruct((1, n * half), F32),
                   jax.ShapeDtypeStruct((rows, half), F32)],
        scratch_shapes=[pltpu.VMEM((lp, width), BF), pltpu.VMEM((k + 32, width), BF), pltpu.VMEM((rows, half), F32)],
        compiler_params=pltpu.CompilerParams(vmem_limit_bytes=40 << 20),
        cost_estimate=pl.CostEstimate(flops=int(8e9), bytes_accessed=int(12e6), transcendentals=0),
        name="project",
    )(echoes, st, s, fc, cr, nr, window)


def border_kernel(n, border_ref, last_ref, win_ref, str_in_ref, vol_in_ref, vol_ref, str_ref, sum_ref, fac_ref):
    frames, half = vol_ref.shape
    rows = last_ref.shape[0]
    k = border_ref.shape[0]
    lp = border_ref.shape[1] - half
    fac_ref[k:, :] = jnp.zeros((128 - k, fac_ref.shape[1]), BF)
    fac_ref[:k, :] = border_ref[...]
    s = fac_ref[:, :lp].astype(F32).T.astype(BF)[:rows]
    done = (n - 1) * half
    parts = jnp.zeros((1, 128), F32)
    for c in range(done // 128):
        at = slice(c * 128, c * 128 + 128)
        parts = parts + str_in_ref[:, at]
    str_ref[:, :done] = str_in_ref[:, :done]
    for c in range(half // CHUNK):
        at = slice(c * CHUNK, (c + 1) * CHUNK)
        low = mm(s, fac_ref[:, lp + c * CHUNK:lp + (c + 1) * CHUNK], NN).astype(BF).astype(F32)
        vol = (last_ref[:, at] + low * win_ref[:, at])[:frames]
        vol_ref[:, at] = vol
        part = jnp.sum(vol * vol, axis=0, keepdims=True) / frames
        str_ref[:, done + c * CHUNK:done + (c + 1) * CHUNK] = part
        for d in range(CHUNK // 128):
            parts = parts + part[:, d * 128:d * 128 + 128]
    sum_ref[0] = parts


def finish(border, last, window, strength, volume, n):
    rows, half = last.shape
    frames = volume.shape[0]
    vm = pl.BlockSpec(memory_space=pltpu.VMEM)
    whole = lambda a: pl.BlockSpec(a.shape, lambda i: (0, 0))
    return pl.pallas_call(
        functools.partial(border_kernel, n),
        grid=(1,),
        in_specs=[whole(border), whole(last), whole(window), whole(strength), pl.BlockSpec(memory_space=pl.ANY)],
        out_specs=[pl.BlockSpec((frames, half), lambda i: (0, n - 1)), whole(strength),
                   pl.BlockSpec((1, 1, 128), lambda i: (0, 0, 0))],
        out_shape=[jax.ShapeDtypeStruct(volume.shape, F32), jax.ShapeDtypeStruct(strength.shape, F32),
                   jax.ShapeDtypeStruct((1, 1, 128), F32)],
        scratch_shapes=[pltpu.VMEM((128, border.shape[1]), BF)],
        input_output_aliases={4: 0},
        compiler_params=pltpu.CompilerParams(vmem_limit_bytes=40 << 20),
        name="finish",
    )(border, last, window, strength, volume)


def reduce_kernel(dims, in_ref, out_ref, near_ref, far_ref, mid_ref, send1, recv1, send2, recv2):
    ny, nz, nx, ng = dims
    plane = ny * nx * ng
    place, core = lax.axis_index("space"), lax.axis_index("grp")
    y, z, x = place // (nz * nx), (place // nx) % nz, place % nx
    me = (y * nx + x) * ng + core

    def near(j):
        other = (me + j) % plane
        return ((other // (nx * ng)) * nz * nx + z * nx + (other // ng) % nx, other % ng)

    def far(j):
        return (y * nz * nx + ((z + j) % nz) * nx + x, core)

    barrier = pltpu.get_barrier_semaphore()

    def greet(peer):
        def body(j, carry):
            pl.semaphore_signal(barrier, inc=1, device_id=peer(j), device_id_type=pl.DeviceIdType.MESH)
            return carry
        return body

    lax.fori_loop(1, plane, greet(near), 0)
    lax.fori_loop(1, nz, greet(far), 0)
    near_ref[me] = in_ref[0]
    pl.semaphore_wait(barrier, plane - 1 + nz - 1)

    def near_copy(j, slot, peer):
        return pltpu.make_async_remote_copy(
            src_ref=in_ref.at[0], dst_ref=near_ref.at[slot], send_sem=send1.at[j], recv_sem=recv1.at[slot],
            device_id=peer, device_id_type=pl.DeviceIdType.MESH)

    def far_copy(j, slot, peer):
        return pltpu.make_async_remote_copy(
            src_ref=mid_ref.at[0], dst_ref=far_ref.at[slot], send_sem=send2.at[j], recv_sem=recv2.at[slot],
            device_id=peer, device_id_type=pl.DeviceIdType.MESH)

    def near_start(j, carry):
        near_copy(j, me, near(j)).start()
        return carry

    def near_wait(j, carry):
        near_copy(j, (me + j) % plane, near(j)).wait()
        return carry

    def far_start(j, carry):
        far_copy(j, z, far(j)).start()
        return carry

    def far_wait(j, carry):
        far_copy(j, (z + j) % nz, far(j)).wait()
        return carry

    lax.fori_loop(1, plane, near_start, 0)
    lax.fori_loop(1, plane, near_wait, 0)
    part = jnp.sum(near_ref[...], axis=0)
    mid_ref[0] = part
    far_ref[z] = part
    lax.fori_loop(1, nz, far_start, 0)
    lax.fori_loop(1, nz, far_wait, 0)
    total = jnp.sum(jnp.sum(far_ref[...], axis=0), axis=1, keepdims=True)
    out_ref[...] = jnp.broadcast_to(total, out_ref.shape)


def total_of(parts, dims):
    ny, nz, nx, ng = dims
    plane = ny * nx * ng
    vm = pl.BlockSpec(memory_space=pltpu.VMEM)
    return pl.pallas_call(
        functools.partial(reduce_kernel, dims),
        in_specs=[vm],
        out_specs=vm,
        out_shape=jax.ShapeDtypeStruct((1, 128), F32),
        scratch_shapes=[pltpu.VMEM((plane, 1, 128), F32), pltpu.VMEM((nz, 1, 128), F32), pltpu.VMEM((1, 1, 128), F32),
                        pltpu.SemaphoreType.DMA((plane,)), pltpu.SemaphoreType.DMA((plane,)),
                        pltpu.SemaphoreType.DMA((nz,)), pltpu.SemaphoreType.DMA((nz,))],
        compiler_params=pltpu.CompilerParams(collective_id=0, has_side_effects=True),
        name="total",
    )(parts)


def shards(dims, echoes, frame_count, clutter_rank, noise_rank, start_basis):
    n, frames, width = echoes.shape
    half = width // 2
    devices = dims[0] * dims[1] * dims[2] * dims[3]
    spot = np.arange(width, dtype=np.float64)
    window = jnp.asarray((np.sin(np.pi * (spot + 0.5) / width) ** 2).astype(np.float32)[None])

    def slot_of(b):
        return (lax.axis_index("space") * dims[3] + lax.axis_index("grp")) * n + b

    st, s, border = subspace(echoes, frame_count, clutter_rank, noise_rank, start_basis, slot_of)
    back = [(d + 1, d) for d in range(devices - 1)]
    border = lax.ppermute(border, ("space", "grp"), back)
    volume, strength, last = project(echoes, st, s, frame_count, clutter_rank, noise_rank, window, slot_of)
    volume, strength, parts = finish(border, last, window, strength, volume, n)
    total = total_of(parts, dims)[0, 0]
    power = strength.reshape(-1) / (total / (devices * n * half) + 1e-6)
    return volume, power


def solution(mesh):
    dims = (4, 8, 4, mesh.shape["grp"])
    both = ("space", "grp")
    return jax.shard_map(
        functools.partial(shards, dims), mesh=mesh,
        in_specs=(P(both, None, None), P(), P(), P(), P()),
        out_specs=(P(None, both), P(both)), check_vma=False)
```

time: 446 us -> 95.6 us (0.21); the launches traced: 438 us -> 95.1 us
  other arithmetic: 212 us -> 0.62 us
  waiting for transfers between devices: 113 us -> 0.01 us
  Pallas kernels: 0 us -> 81 us
  blocking collectives: 44.6 us -> 0 us
  local copies, waits for them, and re-layouts: 34.7 us -> 7.06 us
  matrix products: 19.3 us -> 0 us
  starting transfers between devices: 11.7 us -> 5.1 us
    another operation x22 -> x0, other arithmetic: 196 us -> none  [the longest x13 106 us: filter_block(): factor = jnp.linalg.cholesky(inner_gram)]
    ppermute x3 -> x1, waiting for transfers between devices: 113 us -> 0.01 us  [shards(): border = lax.ppermute(border, ('space', 'grp'), back)]
    pallas_call x0 -> x4, Pallas kernels: none -> 81 us  [the longest x1 52.8 us: subspace(): pl.pallas_call(functools.partial(subspace_kernel, n, w, count_of), grid=(...]
    psum x4 -> x0, blocking collectives: 44.6 us -> none  [one_axis_at_a_time(): return functools.reduce(lax.psum, axes, shard)]
    dot_general x10 -> x0, matrix products: 17 us -> none  [the longest x4 6.56 us: filter_block(): product = jnp.dot(gram_matrix, subspace, precision=lax.Precision.HIGHEST)]
    select_n x4 -> x0, other arithmetic: 8.88 us -> none  [the longest x1 4.25 us: shards(): jnp.where(far_live[:, None, None], empty_blocks, cleaned[low_slot:])]
    transpose x1 -> x0, local copies, waits for them, and re-layouts: 8.29 us -> none  [shards(): volume = jnp.transpose(regions, (1, 0, 2)).reshape(frames_total, -1)]
    ppermute x3 -> x1, starting transfers between devices: 11.7 us -> 5.1 us  [shards(): border = lax.ppermute(border, ('space', 'grp'), back)]
  transfers between devices with their start and end apart: 3 -> 1, of which waited for: 3 -> 0; matrix products, arithmetic and copies ran while one was open for 2% -> 0% of each run, Pallas kernels for 0% -> 8%
where the time goes in v1:
time: 95.6 us; the launch traced here: 95.1 us
  Pallas kernels  81 us (85%)
  local copies, waits for them, and re-layouts  7.06 us (7%)
  starting transfers between devices  5.1 us (5%)
  between operations  1.34 us (1%)
    pallas_call x1, Pallas kernels, subspace(): pl.pallas_call(functools.partial(subspace_kernel, n, w, count_of), grid=(...  52.8 us
    pallas_call x1, Pallas kernels, total_of(): pl.pallas_call(functools.partial(reduce_kernel, dims), in_specs=[vm], out...  19.1 us
    pallas_call x1, Pallas kernels, project(): pl.pallas_call(functools.partial(project_kernel, n, count_of), grid=(n,),...  7.63 us
    unnamed x17, local copies, waits for them, and re-layouts  7.06 us
    ppermute x1, starting transfers between devices, shards(): border = lax.ppermute(border, ('space', 'grp'), back)  5.1 us
  transfers between devices with their start and end apart: 1, of which 0 were waited for; matrix products, arithmetic and copies ran while one was open for 0% of the time, Pallas kernels for 8%

profile of v1, /device:TPU:1, one launch (start us, length us, event | category | flops | bytes accessed | tf_op | source)
XLA Modules:
  0.0 95.1 jit_solution(2015067370278077194)
XLA Ops:
  0.6 0.0 copy-start.4
  0.6 0.0 copy-start.3
  0.7 0.0 copy-start.2
  0.7 0.0 copy-start.1
  0.7 1.7 %copy.9.refs_3_ = f32[300,96]{1,0:T(8,128)} copy(f32[300,96]{0,1:T(8,128)} %param.10) | data formatting | bytes 230400 | tf_op args[4]
  2.4 52.8 %subspace.1 = (bf16[5,128,384]{2,1,0:T(8,128)(2,1)}, bf16[5,384,128]{2,1,0:T(8,128)(2,1)}, bf16[96,1408]{1,0:T(8,128)(2,1)}) custom-call(bf16[5,300,2048]{2,1,0:T(8,128)(2,1)} %echo_ref.3, s32[1280]{0:T(1024)} %fc_ref.1, s32[1280]{0:T(1024)} %cr_ref.1, s32[1280]{0:T(1024)} %nr_ref.1, f32[300,96]{1,0:T(8,128)} %copy.9.refs_3_), custom_call_target="tpu_custom_call" | custom-call | tf_op jit(solution)/shard_map/subspace/pallas_call | solution.py:170
  55.2 5.1 %collective-permute-start = (bf16[96,1408]{1,0:T(8,128)(2,1)}, bf16[96,1408]{1,0:T(8,128)(2,1)S(1)}, u32[]{:S(2)}, u32[]{:S(2)}) collective-permute-start(bf16[96,1408]{1,0:T(8,128)(2,1)} %get-tuple-element.11), channel_id=1, source_target_pairs={{1,0},{2,1},{3,2},{4,3},{5,4},{6,5},{7,6},{8,7},{9,8},{10,9},{11,1... | collective-permute-start | bytes 811016 | tf_op jit(solution)/shard_map/ppermute | solution.py:399
  60.3 0.0 copy-done.4
  60.3 0.0 copy-done.3
  60.3 0.0 copy-done.2
  60.3 0.0 copy-done.1
  60.3 0.0 copy-start
  60.3 2.8 %copy-done = bf16[5,300,2048]{2,1,0:T(8,128)(2,1)S(1)} copy-done((bf16[5,300,2048]{2,1,0:T(8,128)(2,1)S(1)}, bf16[5,300,2048]{2,1,0:T(8,128)(2,1)}, u32[]{:S(2)}) %copy-start) | copy-done | bytes 6144024
  63.1 0.0 copy-start.5
  63.1 1.0 %copy-done.5 = bf16[5,128,384]{2,1,0:T(8,128)(2,1)S(1)} copy-done((bf16[5,128,384]{2,1,0:T(8,128)(2,1)S(1)}, bf16[5,128,384]{2,1,0:T(8,128)(2,1)}, u32[]{:S(2)}) %copy-start.5) | copy-done | bytes 491544
  64.1 0.0 copy-start.6
  64.1 1.0 %copy-done.6 = bf16[5,384,128]{2,1,0:T(8,128)(2,1)S(1)} copy-done((bf16[5,384,128]{2,1,0:T(8,128)(2,1)S(1)}, bf16[5,384,128]{2,1,0:T(8,128)(2,1)}, u32[]{:S(2)}) %copy-start.6) | copy-done | bytes 491544
  65.1 7.6 %project.1 = (f32[300,5120]{1,0:T(8,128)}, f32[1,5120]{1,0:T(1,128)S(1)}, f32[304,1024]{1,0:T(8,128)S(1)}) custom-call(bf16[5,300,2048]{2,1,0:T(8,128)(2,1)S(1)} %copy-done, bf16[5,128,384]{2,1,0:T(8,128)(2,1)S(1)} %copy-done.5, bf16[5,384,128]{2,1,0:T(8,128)(2,1)S(1)} %copy-done.6, s32[1280]{0:T(1024)S(1)} %copy-done.1, s32[1280]{0:T(1024)S(1)} %copy-done.2, ...), custom_call_target="tpu_custom_call" | custom-call | flops 8000000000 | bytes 12000000 | tf_op jit(solution)/shard_map/project/pallas_call | solution.py:241
  72.8 0.0 collective-permute-done.border_ref
  72.8 1.5 %finish.1 = (f32[300,5120]{1,0:T(8,128)}, f32[1,5120]{1,0:T(1,128)S(1)}, f32[1,1,128]{2,1,0:T(1,128)S(1)}) custom-call(bf16[96,1408]{1,0:T(8,128)(2,1)S(1)} %collective-permute-done.border_ref, f32[304,1024]{1,0:T(8,128)S(1)} %get-tuple-element.14.last_ref, f32[1,2048]{1,0:T(1,128)S(1)} %copy-done.4, ...), custom_call_target="tpu_custom_call", output_to_operand_aliasing={{0}: (4, {})} | custom-call | tf_op jit(solution)/shard_map/finish/pallas_call | solution.py:291
  74.3 0.0 copy-start.7
  74.3 0.5 copy-done.7
  74.8 19.1 %total.1 = f32[1,128]{1,0:T(1,128)} custom-call(f32[1,1,128]{2,1,0:T(1,128)} %copy-done.7), custom_call_target="tpu_custom_call" | custom-call | tf_op jit(solution)/shard_map/total/pallas_call | solution.py:374
  94.5 0.6 broadcast_divide_fusion
Async XLA Ops:
  0.6 59.6 %copy-start.4 = (f32[1,2048]{1,0:T(1,128)S(1)}, f32[1,2048]{1,0:T(1,128)}, u32[]{:S(2)}) copy-start(f32[1,2048]{1,0:T(1,128)} %constant.9.clone.win_ref) | copy-start | bytes 24580
  0.6 59.6 %copy-start.3 = (s32[1280]{0:T(1024)S(1)}, s32[1280]{0:T(1024)}, u32[]{:S(2)}) copy-start(s32[1280]{0:T(1024)} %nr_ref.1) | copy-start | bytes 15364
  0.7 59.6 %copy-start.2 = (s32[1280]{0:T(1024)S(1)}, s32[1280]{0:T(1024)}, u32[]{:S(2)}) copy-start(s32[1280]{0:T(1024)} %cr_ref.1) | copy-start | bytes 15364
  0.7 59.6 %copy-start.1 = (s32[1280]{0:T(1024)S(1)}, s32[1280]{0:T(1024)}, u32[]{:S(2)}) copy-start(s32[1280]{0:T(1024)} %fc_ref.1) | copy-start | bytes 15364
  55.2 17.6 %collective-permute-start = (bf16[96,1408]{1,0:T(8,128)(2,1)}, bf16[96,1408]{1,0:T(8,128)(2,1)S(1)}, u32[]{:S(2)}, u32[]{:S(2)}) collective-permute-start(bf16[96,1408]{1,0:T(8,128)(2,1)} %get-tuple-element.11), channel_id=1, source_target_pairs={{1,0},{2,1},{3,2},{4,3},{5,4},{6,5},{7,6},{8,7},{9,8},{10,9},{11,1... | collective-permute-start | bytes 811016 | tf_op jit(solution)/shard_map/ppermute | solution.py:399
  60.3 2.8 %copy-start = (bf16[5,300,2048]{2,1,0:T(8,128)(2,1)S(1)}, bf16[5,300,2048]{2,1,0:T(8,128)(2,1)}, u32[]{:S(2)}) copy-start(bf16[5,300,2048]{2,1,0:T(8,128)(2,1)} %echo_ref.3) | copy-start | bytes 18432004
  63.1 1.0 %copy-start.5 = (bf16[5,128,384]{2,1,0:T(8,128)(2,1)S(1)}, bf16[5,128,384]{2,1,0:T(8,128)(2,1)}, u32[]{:S(2)}) copy-start(bf16[5,128,384]{2,1,0:T(8,128)(2,1)} %get-tuple-element.12.st_ref) | copy-start | bytes 1474564
  64.1 1.0 %copy-start.6 = (bf16[5,384,128]{2,1,0:T(8,128)(2,1)S(1)}, bf16[5,384,128]{2,1,0:T(8,128)(2,1)}, u32[]{:S(2)}) copy-start(bf16[5,384,128]{2,1,0:T(8,128)(2,1)} %get-tuple-element.13.s_ref) | copy-start | bytes 1474564
  74.3 0.5 copy-start.7

commit v2 on v1

--- a/solution.py
+++ b/solution.py
@@ -25,6 +25,10 @@
     rest = a - hi.astype(F32)
     mid = rest.astype(BF)
     return hi, mid, (rest - mid.astype(F32)).astype(BF)
+
+def spread(tile, row):
+    return jnp.take_along_axis(tile, jnp.full((8, 128), row, jnp.int32), axis=0)
+
 
 def eliminate(a_ref, s_ref, blocks, k, w, between):
     tiles = k // 8
@@ -35,19 +39,20 @@
         t0, r0 = j0 // 8, j0 % 8
         inside = (lane >= j0) & (lane < j0 + w)
         between(p)
-        cols, diag = {}, {}
+        cols, diag, tile = {}, {}, {}
         for b in blocks:
             for t in range(t0, tiles):
-                tile = a_ref[b, 8 * t:8 * t + 8, :]
-                for q in range(w):
-                    cols[b, q, t] = jnp.broadcast_to(tile[:, j0 + q:j0 + q + 1], (8, 128))
-                if t == t0:
-                    diag[b] = jnp.where(inside, 0.0, tile)
+                tile[b, t] = a_ref[b, 8 * t:8 * t + 8, :]
+            diag[b] = jnp.where(inside, 0.0, tile[b, t0])
+        for q in range(w):
+            for b in blocks:
+                for t in range(t0, tiles):
+                    cols[b, q, t] = jnp.broadcast_to(tile[b, t][:, j0 + q:j0 + q + 1], (8, 128))
         facs, rows, scal = {}, {}, {}
         for q in range(w):
             r, j = r0 + q, j0 + q
             for b in blocks:
-                pivot = jnp.broadcast_to(cols[b, q, t0][r:r + 1, :], (8, 128))
+                pivot = spread(cols[b, q, t0], r)
                 inv = 1.0 / pivot
                 root = lax.rsqrt(pivot)
                 scal[b] = root if q == 0 else jnp.where(sub == r, root, scal[b])
@@ -55,10 +60,10 @@
                     f = cols[b, q, t] * inv
                     facs[b, q, t] = jnp.where(sub > r, f, 0.0) if t == t0 else f
                 for q2 in range(q + 1, w):
-                    m = jnp.broadcast_to(cols[b, q2, t0][r:r + 1, :], (8, 128))
+                    m = spread(cols[b, q2, t0], r)
                     for t in range(t0, tiles):
                         cols[b, q2, t] = cols[b, q2, t] - facs[b, q, t] * m
-                row = jnp.broadcast_to(diag[b][r:r + 1, :], (8, 128))
+                row = spread(diag[b], r)
                 row = jnp.where(lane == j, 1.0, jnp.where((lane > j) & (lane < j0 + w), 0.0, row))
                 rows[b, q] = row
                 diag[b] = diag[b] - facs[b, q, t0] * row
@@ -66,25 +71,27 @@
             a_ref[b, 8 * t0:8 * t0 + 8, :] = diag[b]
             s_ref[b, j0:j0 + w, :] = scal[b][r0:r0 + w, :]
             for t in range(t0 + 1, tiles):
-                tile = jnp.where(inside, 0.0, a_ref[b, 8 * t:8 * t + 8, :])
+                rest = jnp.where(inside, 0.0, tile[b, t])
                 for q in range(w):
-                    tile = tile - facs[b, q, t] * rows[b, q]
-                a_ref[b, 8 * t:8 * t + 8, :] = tile
+                    rest = rest - facs[b, q, t] * rows[b, q]
+                a_ref[b, 8 * t:8 * t + 8, :] = rest
 
 
 def subspace_kernel(n, w, count_of, echo_ref, *refs):
     (fc_ref, cr_ref, nr_ref, start_ref, st_ref, s_out_ref, border_ref, x_ref, first_ref, gh_ref, gl_ref, p_ref, y_ref, a_ref, s_ref) = refs
     step = pl.program_id(0)
-    frames, k = start_ref.shape
+    k, frames = start_ref.shape
     lp = gh_ref.shape[2]
 
     @pl.when(step == 0)
     def _():
-        x_ref[...] = jnp.zeros_like(x_ref)
-        gh_ref[...] = jnp.zeros_like(gh_ref)
-        gl_ref[...] = jnp.zeros_like(gl_ref)
-        p_ref[...] = jnp.zeros_like(p_ref)
-        y_ref[...] = jnp.zeros_like(y_ref)
+        top = frames // 16 * 16
+        x_ref[top:, :] = jnp.zeros((lp - top, x_ref.shape[1]), BF)
+        gh_ref[:, top:, :] = jnp.zeros((n, lp - top, lp), BF)
+        gl_ref[:, top:, :] = jnp.zeros((n, lp - top, lp), BF)
+        p_ref[0] = jnp.zeros_like(p_ref[0])
+        p_ref[:, k:, :] = jnp.zeros((n, 128 - k, lp), F32)
+        y_ref[:, k:, :] = jnp.zeros((n, 128 - k, lp), F32)
 
     total = fc_ref[count_of(step)]
     row = lax.broadcasted_iota(jnp.int32, (frames, 1), 0)
@@ -106,11 +113,8 @@
     @pl.when(step == n - 1)
     def _():
         blocks = range(n)
-        s0 = start_ref[...]
-        s0 = jnp.concatenate([s0, jnp.zeros((frames, 128 - k), F32)], axis=1)
-        s0 = jnp.concatenate([s0, jnp.zeros((lp - frames, 128), F32)], axis=0)
-        s0t = s0.T
-        sh, sl = split(s0t)
+        p_ref[0, :k, :frames] = start_ref[...]
+        sh, sl = split(p_ref[0])
         for b in blocks:
             p_ref[b, :, :] = mm(sh, gh_ref[b], NN) + mm(sh, gl_ref[b], NN) + mm(sl, gh_ref[b], NN)
 
@@ -163,7 +167,7 @@
 
 def subspace(echoes, fc, cr, nr, start, count_of, w=4):
     n, frames, width = echoes.shape
-    k = start.shape[1]
+    k = start.shape[0]
     lp = -(-frames // 128) * 128
     smem = pl.BlockSpec(memory_space=pltpu.SMEM)
     edge = (k, lp + width // 2)
@@ -172,7 +176,7 @@
         grid=(n,),
         in_specs=[pl.BlockSpec((1, frames, width), lambda i: (i, 0, 0)),
                   smem, smem, smem,
-                  pl.BlockSpec((frames, k), lambda i: (0, 0))],
+                  pl.BlockSpec((k, frames), lambda i: (0, 0))],
         out_specs=[pl.BlockSpec((n, 128, lp), lambda i: (0, 0, 0)),
                    pl.BlockSpec((n, lp, 128), lambda i: (0, 0, 0)),
                    pl.BlockSpec(edge, lambda i: (0, 0))],
@@ -251,7 +255,7 @@
         out_shape=[jax.ShapeDtypeStruct((frames, n * half), F32), jax.ShapeDtypeStruct((1, n * half), F32),
                    jax.ShapeDtypeStruct((rows, half), F32)],
         scratch_shapes=[pltpu.VMEM((lp, width), BF), pltpu.VMEM((k + 32, width), BF), pltpu.VMEM((rows, half), F32)],
-        compiler_params=pltpu.CompilerParams(vmem_limit_bytes=40 << 20),
+        compiler_params=pltpu.CompilerParams(vmem_limit_bytes=62 << 20),
         cost_estimate=pl.CostEstimate(flops=int(8e9), bytes_accessed=int(12e6), transcendentals=0),
         name="project",
     )(echoes, st, s, fc, cr, nr, window)
@@ -394,7 +398,7 @@
     def slot_of(b):
         return (lax.axis_index("space") * dims[3] + lax.axis_index("grp")) * n + b
 
-    st, s, border = subspace(echoes, frame_count, clutter_rank, noise_rank, start_basis, slot_of)
+    st, s, border = subspace(echoes, frame_count, clutter_rank, noise_rank, start_basis.T, slot_of)
     back = [(d + 1, d) for d in range(devices - 1)]
     border = lax.ppermute(border, ("space", "grp"), back)
     volume, strength, last = project(echoes, st, s, frame_count, clutter_rank, noise_rank, window, slot_of)

time: 95.6 us -> 76.1 us (0.80)
  Pallas kernels: 81 us -> 66.1 us
  local copies, waits for them, and re-layouts: 7.06 us -> 2.53 us
    pallas_call x1, Pallas kernels: 52.8 us -> 35.9 us  [subspace(): pl.pallas_call(functools.partial(subspace_kernel, n, w, count_of), grid=(...]
    unnamed x17 -> x8, local copies, waits for them, and re-layouts: 7.06 us -> 2.53 us
    pallas_call x1, Pallas kernels: 7.63 us -> 9.62 us  [project(): pl.pallas_call(functools.partial(project_kernel, n, count_of), grid=(n,),...]
  transfers between devices with their start and end apart: 1 -> 1, of which waited for: 0 -> 0; matrix products, arithmetic and copies ran while one was open for 0% -> 0% of each run, Pallas kernels for 8% -> 13%
where the time goes in v2:
time: 76.1 us; the launch traced here: 75.6 us
  Pallas kernels  66.1 us (87%)
  starting transfers between devices  5.1 us (7%)
  local copies, waits for them, and re-layouts  2.53 us (3%)
  between operations  1.24 us (2%)
    pallas_call x1, Pallas kernels, subspace(): pl.pallas_call(functools.partial(subspace_kernel, n, w, count_of), grid=(...  35.9 us
    pallas_call x1, Pallas kernels, total_of(): pl.pallas_call(functools.partial(reduce_kernel, dims), in_specs=[vm], out...  19 us
    pallas_call x1, Pallas kernels, project(): pl.pallas_call(functools.partial(project_kernel, n, count_of), grid=(n,),...  9.62 us
    ppermute x1, starting transfers between devices, shards(): border = lax.ppermute(border, ('space', 'grp'), back)  5.1 us
    unnamed x8, local copies, waits for them, and re-layouts  2.53 us
  transfers between devices with their start and end apart: 1, of which 0 were waited for; matrix products, arithmetic and copies ran while one was open for 0% of the time, Pallas kernels for 13%

profile of v2, /device:TPU:1, one launch (start us, length us, event | category | flops | bytes accessed | tf_op | source)
XLA Modules:
  0.0 75.6 jit_solution(12749278472290868564)
XLA Ops:
  0.6 35.9 %subspace.1 = (bf16[5,128,384]{2,1,0:T(8,128)(2,1)}, bf16[5,384,128]{2,1,0:T(8,128)(2,1)}, bf16[96,1408]{1,0:T(8,128)(2,1)}) custom-call(bf16[5,300,2048]{2,1,0:T(8,128)(2,1)} %echo_ref.3, s32[1280]{0:T(1024)} %fc_ref.1, s32[1280]{0:T(1024)} %cr_ref.1, s32[1280]{0:T(1024)} %nr_ref.1, f32[96,300]{1,0:T(8,128)} %bitcast.4), custom_call_target="tpu_custom_call" | custom-call | tf_op jit(solution)/shard_map/subspace/pallas_call | solution.py:174
  36.5 5.1 %collective-permute-start = (bf16[96,1408]{1,0:T(8,128)(2,1)}, bf16[96,1408]{1,0:T(8,128)(2,1)S(1)}, u32[]{:S(2)}, u32[]{:S(2)}) collective-permute-start(bf16[96,1408]{1,0:T(8,128)(2,1)} %get-tuple-element.11), channel_id=1, source_target_pairs={{1,0},{2,1},{3,2},{4,3},{5,4},{6,5},{7,6},{8,7},{9,8},{10,9},{11,1... | collective-permute-start | bytes 811016 | tf_op jit(solution)/shard_map/ppermute | solution.py:403
  41.6 0.0 copy-start.2
  41.7 9.6 %project.1 = (f32[300,5120]{1,0:T(8,128)}, f32[1,5120]{1,0:T(1,128)}, f32[304,1024]{1,0:T(8,128)}) custom-call(bf16[5,300,2048]{2,1,0:T(8,128)(2,1)} %echo_ref.3, bf16[5,128,384]{2,1,0:T(8,128)(2,1)} %get-tuple-element.12.st_ref, bf16[5,384,128]{2,1,0:T(8,128)(2,1)} %get-tuple-element.13.s_ref, s32[1280]{0:T(1024)} %fc_ref.1, s32[1280]{0:T(1024)} %cr_ref.1, ...), custom_call_target="tpu_custom_call" | custom-call | flops 8000000000 | bytes 12000000 | tf_op jit(solution)/shard_map/project/pallas_call | solution.py:245
  51.3 0.0 collective-permute-done.border_ref
  51.3 0.0 copy-done.2
  51.3 0.0 copy-start
  51.3 1.3 %copy-done = f32[304,1024]{1,0:T(8,128)S(1)} copy-done((f32[304,1024]{1,0:T(8,128)S(1)}, f32[304,1024]{1,0:T(8,128)}, u32[]{:S(2)}) %copy-start) | copy-done | bytes 1245208
  52.6 0.0 copy-start.1
  52.6 0.7 copy-done.1
  53.3 1.5 %finish.1 = (f32[300,5120]{1,0:T(8,128)}, f32[1,5120]{1,0:T(1,128)S(1)}, f32[1,1,128]{2,1,0:T(1,128)S(1)}) custom-call(bf16[96,1408]{1,0:T(8,128)(2,1)S(1)} %collective-permute-done.border_ref, f32[304,1024]{1,0:T(8,128)S(1)} %copy-done, f32[1,2048]{1,0:T(1,128)S(1)} %copy-done.2, f32[1,5120]{1,0:T(1,128)S(1)} %copy-done.1, ...), custom_call_target="tpu_custom_call", output_to_operand_aliasing={{0}: (4, {})} | custom-call | tf_op jit(solution)/shard_map/finish/pallas_call | solution.py:295
  54.8 0.0 copy-start.3
  54.8 0.5 copy-done.3
  55.3 19.0 %total.1 = f32[1,128]{1,0:T(1,128)} custom-call(f32[1,1,128]{2,1,0:T(1,128)} %copy-done.3), custom_call_target="tpu_custom_call" | custom-call | tf_op jit(solution)/shard_map/total/pallas_call | solution.py:378
  74.9 0.6 broadcast_divide_fusion
Async XLA Ops:
  36.5 14.7 %collective-permute-start = (bf16[96,1408]{1,0:T(8,128)(2,1)}, bf16[96,1408]{1,0:T(8,128)(2,1)S(1)}, u32[]{:S(2)}, u32[]{:S(2)}) collective-permute-start(bf16[96,1408]{1,0:T(8,128)(2,1)} %get-tuple-element.11), channel_id=1, source_target_pairs={{1,0},{2,1},{3,2},{4,3},{5,4},{6,5},{7,6},{8,7},{9,8},{10,9},{11,1... | collective-permute-start | bytes 811016 | tf_op jit(solution)/shard_map/ppermute | solution.py:403
  41.6 9.7 %copy-start.2 = (f32[1,2048]{1,0:T(1,128)S(1)}, f32[1,2048]{1,0:T(1,128)}, u32[]{:S(2)}) copy-start(f32[1,2048]{1,0:T(1,128)} %constant.9.clone.win_ref) | copy-start | bytes 24580
  51.3 1.3 %copy-start = (f32[304,1024]{1,0:T(8,128)S(1)}, f32[304,1024]{1,0:T(8,128)}, u32[]{:S(2)}) copy-start(f32[304,1024]{1,0:T(8,128)} %get-tuple-element.14.last_ref) | copy-start | bytes 3735556
  52.6 0.7 copy-start.1
  54.8 0.5 copy-start.3

commit v3 on v2

v3 whole, which is shorter than its diff:
```python
import functools
import numpy as np
import jax, jax.numpy as jnp
from jax import lax
from jax.experimental import pallas as pl
from jax.experimental.pallas import tpu as pltpu
from jax.sharding import PartitionSpec as P

F32, BF = jnp.float32, jnp.bfloat16
ITERS = 4
CHUNK = 512
EARLY = 0

NT = (((1,), (1,)), ((), ()))
NN = (((1,), (0,)), ((), ()))

def mm(a, b, dims):
    return lax.dot_general(a, b, dims, preferred_element_type=F32)

def split(a):
    hi = a.astype(BF)
    return hi, (a - hi.astype(F32)).astype(BF)

def split3(a):
    hi = a.astype(BF)
    rest = a - hi.astype(F32)
    mid = rest.astype(BF)
    return hi, mid, (rest - mid.astype(F32)).astype(BF)

def spread(tile, row):
    return jnp.take_along_axis(tile, jnp.full((8, 128), row, jnp.int32), axis=0)


GAP = 64


def eliminate(m_ref, s_ref, pairs, k, between):
    tiles = k // 8
    sub = lax.broadcasted_iota(jnp.int32, (8, 128), 0)
    place = lax.broadcasted_iota(jnp.int32, (8, 128), 1)
    lane = place & (GAP - 1)
    for p in range(tiles):
        j0 = 8 * p
        inside = (lane >= j0) & (lane < j0 + 8)
        eye = jnp.where(lane == j0 + sub, 1.0, 0.0)
        between(p)
        cols, diag, tile, inverses, pivots = {}, {}, {}, {}, {}
        for b in pairs:
            for t in range(p, tiles):
                tile[b, t] = m_ref[b, 8 * t:8 * t + 8, :]
            diag[b] = jnp.where(inside, eye, tile[b, p])
        for q in range(8):
            pick = place - lane + (j0 + q)
            for b in pairs:
                for t in range(p, tiles):
                    cols[b, q, t] = jnp.take_along_axis(tile[b, t], pick, axis=1)
        for q in range(8):
            for b in pairs:
                pivot = spread(cols[b, q, p], q)
                inv = 1.0 / pivot
                pivots[b] = pivot if q == 0 else jnp.where(sub == q, pivot, pivots[b])
                inverses[b] = inv if q == 0 else jnp.where(sub == q, inv, inverses[b])
                if q < 7:
                    f = jnp.where(sub > q, cols[b, q, p] * inv, 0.0)
                    for q2 in range(q + 1, 8):
                        cols[b, q2, p] = cols[b, q2, p] - f * spread(cols[b, q2, p], q)
                    diag[b] = diag[b] - f * spread(diag[b], q)
        for b in pairs:
            m_ref[b, j0:j0 + 8, :] = diag[b]
            s_ref[b, j0:j0 + 8, :] = lax.rsqrt(pivots[b])
        if p == tiles - 1:
            break
        for b in pairs:
            solved = diag[b] * inverses[b]
            for q in range(7, 0, -1):
                g = jnp.where(sub < q, cols[b, q, p] * inverses[b], 0.0)
                solved = solved - g * spread(solved, q)
            rows = [spread(solved, q) for q in range(8)]
            for t in range(p + 1, tiles):
                rest = jnp.where(inside, 0.0, tile[b, t])
                for q in range(8):
                    rest = rest - cols[b, q, t] * rows[q]
                m_ref[b, 8 * t:8 * t + 8, :] = rest


def mm3(a, b, dims=NN):
    (ah, al), (bh, bl) = a, b
    m = ah.shape[0]
    first = mm(jnp.concatenate([ah, al], axis=0), bh, dims)
    return first[:m] + (first[m:] + mm(ah, bl, dims))


def mm6(a, b, dims=NN):
    (ah, am, al), (bh, bm, bl) = a, b
    m = ah.shape[0]
    first = mm(jnp.concatenate([ah, am, al], axis=0), bh, dims)
    second = mm(jnp.concatenate([ah, am], axis=0), bm, dims)
    return first[:m] + (first[m:2 * m] + second[:m]) + (second[m:] + first[2 * m:] + mm(ah, bl, dims))


def both(parts, h):
    return tuple(jnp.concatenate([a[:h], a[GAP:GAP + h]], axis=0) for a in parts)


def chosen(rows, h):
    lane = lax.broadcasted_iota(jnp.int32, (h, 128), 1)
    return jnp.where(lane < GAP, rows[:h], rows[h:])


def stacked(x, pad):
    lane = lax.broadcasted_iota(jnp.int32, x.shape, 1)
    first, second = jnp.where(lane < GAP, x, 0.0), jnp.where(lane < GAP, 0.0, x)
    if not pad:
        return jnp.concatenate([first, second], axis=0)
    zero = jnp.zeros((pad, 128), F32)
    return jnp.concatenate([first, zero, second, zero], axis=0)


def subspace_kernel(n, count_of, echo_ref, *refs):
    (fc_ref, cr_ref, nr_ref, start_ref, st_ref, s_out_ref, border_ref, x_ref, gh_ref, gl_ref, p_ref, y_ref, a_ref, s_ref) = refs
    step = pl.program_id(0)
    k, frames = start_ref.shape
    lp = gh_ref.shape[2]

    @pl.when(step == 0)
    def _():
        top = frames // 16 * 16
        gh_ref[:, top:, :] = jnp.zeros((n, lp - top, lp), BF)
        gl_ref[:, top:, :] = jnp.zeros((n, lp - top, lp), BF)

    total = fc_ref[count_of(step)]
    row = lax.broadcasted_iota(jnp.int32, (frames, 1), 0)
    top = frames // 16 * 16
    x_ref[step, top:, :] = jnp.zeros((lp - top, x_ref.shape[2]), BF)
    x_ref[step, :frames, :] = jnp.where(row < total, echo_ref[0], jnp.zeros((), BF))
    x = x_ref[step]
    rows, cut = -(-frames // 16) * 16, frames // 256 * 256
    left = mm(x[:rows], x[:cut], NT)
    right = mm(x[cut:rows], x[cut:lp], NT)
    low = jnp.concatenate([left[cut:], jnp.zeros((lp - rows, cut), F32)], axis=0)
    g = jnp.concatenate([left, jnp.concatenate([low.T, right], axis=0)], axis=1)


    gr = lax.broadcasted_iota(jnp.int32, g.shape, 0)
    gc = lax.broadcasted_iota(jnp.int32, g.shape, 1)
    g = g + jnp.where((gr == gc) & (gr >= total) & (gr < frames), 1.0, 0.0)
    hi, lo = split(g)
    gh_ref[step, :g.shape[0], :] = hi
    gl_ref[step, :g.shape[0], :] = lo

    @pl.when(step == n - 1)
    def _():
        blocks = range(n)
        half = k // 2
        pairs = [(b, min(b + 1, n - 1)) for b in range(0, n, 2)]
        spots = [[(i, e * GAP) for i, pair in enumerate(pairs) for e in (0, 1) if pair[e] == b] for b in range(n)]

        def place(ref, b, value):
            for i, at in spots[b]:
                ref[i, 0, at:at + half, :] = value[:half]
                ref[i, 1, at:at + half, :] = value[half:]

        y_ref[0, 0, :, :] = jnp.zeros((128, lp), F32)
        y_ref[0, 0, :k, :frames] = start_ref[...]
        start = split(y_ref[0, 0])
        y_ref[...] = jnp.zeros_like(y_ref)
        p_ref[...] = jnp.zeros_like(p_ref)
        for b in range(n):
            place(p_ref, b, mm3(start, (gh_ref[b], gl_ref[b]))[:k])

        def forward(b):
            i, at = spots[b][0]
            p = jnp.concatenate([p_ref[i, 0, at:at + half, :], p_ref[i, 1, at:at + half, :]], axis=0)
            place(y_ref, b, mm3(split(p), (gh_ref[b], gl_ref[b])))

        count = range(len(pairs))

        def leaf(mats, between):
            for i in count:
                a_ref[i, :, :] = mats[i]
            eliminate(a_ref, s_ref, count, half, between)
            out = []
            for i in count:
                lower = a_ref[i]
                ri = lax.broadcasted_iota(jnp.int32, lower.shape, 0)
                ci = lax.broadcasted_iota(jnp.int32, lower.shape, 1) & (GAP - 1)
                out.append(jnp.where(ci < ri, lower, jnp.where(ci == ri, 1.0, 0.0)) * s_ref[i])
            return out

        def inverse(moves):
            z = [[split3(p_ref[i, 0]), split3(p_ref[i, 1])] for i in count]
            c11 = [chosen(mm6(both(z[i][0], half), z[i][0], NT), half) for i in count]
            c12, c22 = {}, {}

            def others(i):
                rows = tuple(jnp.concatenate(parts, axis=0) for parts in zip(both(z[i][0], half), both(z[i][1], half)))
                c = mm6(rows, z[i][1], NT)
                c12[i], c22[i] = chosen(c[:k], half), chosen(c[k:], half)

            panels = half // 8
            first = [functools.partial(others, i) for i in count] + moves[:EARLY]

            def run(some, last):
                plan = {}
                for e, m in enumerate(some):
                    plan.setdefault(e * last // max(len(some), 1), []).append(m)
                return lambda p: [m() for m in plan.get(p, [])]

            w11 = leaf(c11, run(first, panels - 1))
            fill = jnp.zeros((128 - half, 128), F32)
            u, ut = [], []
            for i in count:
                x = mm6(split3(w11[i]), split3(stacked(c12[i], GAP - half)))
                x = jnp.concatenate([x, fill], axis=0)
                u.append(x)
                ut.append(both(split3(x.T), half))
            w22 = leaf([c22[i] - chosen(mm6(ut[i], split3(u[i])), half) for i in count],
                       run(moves[EARLY:], panels - 1))
            out = []
            for i in count:
                t = chosen(mm3(ut[i][:2], split(jnp.concatenate([w11[i], fill], axis=0))), half)
                w21 = -mm3(split(w22[i]), split(stacked(t, GAP - half)))
                top = jnp.concatenate([stacked(w11[i], 0), jnp.zeros((k, 128), F32)], axis=1)
                low = jnp.concatenate([stacked(w21, 0), stacked(w22[i], 0)], axis=1)
                out.append(split(jnp.concatenate([top, low], axis=0)))
            return out

        def apply(factors, ref, i):
            rows = mm3(factors, split(jnp.concatenate([ref[i, 0], ref[i, 1]], axis=0)))
            return rows[:k], rows[k:]

        def body(i, carry):
            factors = inverse([functools.partial(forward, b) for b in range(n)])
            for i in count:
                top, low = apply(factors[i], y_ref, i)
                for e in (0, 1):
                    p_ref[i, 0, e * GAP:e * GAP + half, :] = top[e * half:(e + 1) * half]
                    p_ref[i, 1, e * GAP:e * GAP + half, :] = low[e * half:(e + 1) * half]
            return carry

        lax.fori_loop(0, ITERS - 1, body, 0)
        factors = inverse([])
        fill = jnp.zeros((128 - k, lp), F32)
        for i in count:
            top, low = apply(factors[i], p_ref, i)
            for e in (0, 1):
                b = pairs[i][e]
                if spots[b][0] == (i, e * GAP):
                    rows = slice(e * half, (e + 1) * half)
                    st = jnp.concatenate([top[rows], low[rows], fill], axis=0)
                    st_ref[b, :, :] = st.astype(BF)
                    s_out_ref[b, :, :] = st.T.astype(BF)
        slot = count_of(0)
        band = band_of(k, cr_ref[slot], nr_ref[slot])
        basis = st_ref[0, :k, :]
        border_ref[:, :lp] = basis
        border_ref[:, lp:] = (mm(basis, x_ref[0, :, :x_ref.shape[2] // 2], NN) * band).astype(BF)


def subspace(echoes, fc, cr, nr, start, count_of):
    n, frames, width = echoes.shape
    k = start.shape[0]
    lp = -(-frames // 128) * 128
    half_n = -(-n // 2)
    smem = pl.BlockSpec(memory_space=pltpu.SMEM)
    edge = (k, lp + width // 2)
    return pl.pallas_call(
        functools.partial(subspace_kernel, n, count_of),
        grid=(n,),
        in_specs=[pl.BlockSpec((1, frames, width), lambda i: (i, 0, 0)),
                  smem, smem, smem,
                  pl.BlockSpec((k, frames), lambda i: (0, 0))],
        out_specs=[pl.BlockSpec((n, 128, lp), lambda i: (0, 0, 0)),
                   pl.BlockSpec((n, lp, 128), lambda i: (0, 0, 0)),
                   pl.BlockSpec(edge, lambda i: (0, 0)),
                   pl.BlockSpec((n, lp, width), lambda i: (0, 0, 0))],
        out_shape=[jax.ShapeDtypeStruct((n, 128, lp), BF), jax.ShapeDtypeStruct((n, lp, 128), BF),
                   jax.ShapeDtypeStruct(edge, BF), jax.ShapeDtypeStruct((n, lp, width), BF)],
        scratch_shapes=[pltpu.VMEM((n, lp, lp), BF), pltpu.VMEM((n, lp, lp), BF),
                        pltpu.VMEM((half_n, 2, 128, lp), F32), pltpu.VMEM((half_n, 2, 128, lp), F32),
                        pltpu.VMEM((half_n, k // 2, 128), F32), pltpu.VMEM((half_n, k // 2, 128), F32)],
        compiler_params=pltpu.CompilerParams(vmem_limit_bytes=32 << 20),
        name="subspace",
    )(echoes, fc, cr, nr, start)


def project_kernel(n, frames, count_of, x_ref, st_ref, s_ref, cr_ref, nr_ref, win_ref, vol_ref, str_ref, last_ref,
                   coef_ref, prev_ref):
    step = pl.program_id(0)
    width = x_ref.shape[2]
    half = width // 2
    k = coef_ref.shape[0] - 32
    rows = prev_ref.shape[0]

    @pl.when(step == 0)
    def _():
        coef_ref[...] = jnp.zeros_like(coef_ref)

    slot = count_of(step)
    band = band_of(k, cr_ref[slot], nr_ref[slot])
    st, s = st_ref[0, :k, :], s_ref[0, :rows, :]
    for c in range(width // CHUNK):
        at = slice(c * CHUNK, (c + 1) * CHUNK)
        coef_ref[:k, at] = (mm(st, x_ref[0, :, at], NN) * band).astype(BF)

    @pl.when(step > 0)
    def _():
        for c in range(half // CHUNK):
            at = slice(c * CHUNK, (c + 1) * CHUNK)
            low = mm(s, coef_ref[:, at], NN).astype(BF).astype(F32)
            vol = (prev_ref[:, at] + low * win_ref[:, at])[:frames]
            vol_ref[:, at] = vol
            str_ref[:, at] = jnp.sum(vol * vol, axis=0, keepdims=True) / frames

    for c in range(half // CHUNK):
        at, up = slice(c * CHUNK, (c + 1) * CHUNK), slice(half + c * CHUNK, half + (c + 1) * CHUNK)
        prev_ref[:, at] = mm(s, coef_ref[:, up], NN).astype(BF).astype(F32) * win_ref[:, up]

    @pl.when(step == n - 1)
    def _():
        last_ref[...] = prev_ref[...]


def band_of(k, low, high):
    col = lax.broadcasted_iota(jnp.int32, (k, 1), 0)
    return jnp.where((col >= low) & (col < high), 1.0, 0.0)


def project(masked, frames, st, s, cr, nr, window, count_of):
    n, _, width = masked.shape
    half, lp, k = width // 2, st.shape[2], st.shape[1] - 32
    rows = -(-frames // 16) * 16
    smem = pl.BlockSpec(memory_space=pltpu.SMEM)
    after = lambda i: (0, jnp.maximum(i - 1, 0))
    return pl.pallas_call(
        functools.partial(project_kernel, n, frames, count_of),
        grid=(n,),
        in_specs=[pl.BlockSpec((1, lp, width), lambda i: (i, 0, 0)),
                  pl.BlockSpec((1, 128, lp), lambda i: (i, 0, 0)),
                  pl.BlockSpec((1, lp, 128), lambda i: (i, 0, 0)),
                  smem, smem,
                  pl.BlockSpec((1, width), lambda i: (0, 0))],
        out_specs=[pl.BlockSpec((frames, half), after), pl.BlockSpec((1, half), after),
                   pl.BlockSpec((rows, half), lambda i: (0, 0))],
        out_shape=[jax.ShapeDtypeStruct((frames, n * half), F32), jax.ShapeDtypeStruct((1, n * half), F32),
                   jax.ShapeDtypeStruct((rows, half), F32)],
        scratch_shapes=[pltpu.VMEM((k + 32, width), BF), pltpu.VMEM((rows, half), F32)],
        compiler_params=pltpu.CompilerParams(vmem_limit_bytes=32 << 20),
        cost_estimate=pl.CostEstimate(flops=int(8e9), bytes_accessed=int(12e6), transcendentals=0),
        name="project",
    )(masked, st, s, cr, nr, window)


def border_kernel(n, border_ref, last_ref, win_ref, str_in_ref, vol_in_ref, vol_ref, str_ref, sum_ref, fac_ref):
    frames, half = vol_ref.shape
    rows = last_ref.shape[0]
    k = border_ref.shape[0]
    lp = border_ref.shape[1] - half
    fac_ref[k:, :] = jnp.zeros((128 - k, fac_ref.shape[1]), BF)
    fac_ref[:k, :] = border_ref[...]
    s = fac_ref[:, :lp].astype(F32).T.astype(BF)[:rows]
    done = (n - 1) * half
    parts = jnp.zeros((1, 128), F32)
    for c in range(done // 128):
        at = slice(c * 128, c * 128 + 128)
        parts = parts + str_in_ref[:, at]
    str_ref[:, :done] = str_in_ref[:, :done]
    for c in range(half // CHUNK):
        at = slice(c * CHUNK, (c + 1) * CHUNK)
        low = mm(s, fac_ref[:, lp + c * CHUNK:lp + (c + 1) * CHUNK], NN).astype(BF).astype(F32)
        vol = (last_ref[:, at] + low * win_ref[:, at])[:frames]
        vol_ref[:, at] = vol
        part = jnp.sum(vol * vol, axis=0, keepdims=True) / frames
        str_ref[:, done + c * CHUNK:done + (c + 1) * CHUNK] = part
        for d in range(CHUNK // 128):
            parts = parts + part[:, d * 128:d * 128 + 128]
    sum_ref[0] = parts


def finish(border, last, window, strength, volume, n):
    rows, half = last.shape
    frames = volume.shape[0]
    vm = pl.BlockSpec(memory_space=pltpu.VMEM)
    whole = lambda a: pl.BlockSpec(a.shape, lambda i: (0, 0))
    return pl.pallas_call(
        functools.partial(border_kernel, n),
        grid=(1,),
        in_specs=[whole(border), whole(last), whole(window), whole(strength), pl.BlockSpec(memory_space=pl.ANY)],
        out_specs=[pl.BlockSpec((frames, half), lambda i: (0, n - 1)), whole(strength),
                   pl.BlockSpec((1, 1, 128), lambda i: (0, 0, 0))],
        out_shape=[jax.ShapeDtypeStruct(volume.shape, F32), jax.ShapeDtypeStruct(strength.shape, F32),
                   jax.ShapeDtypeStruct((1, 1, 128), F32)],
        scratch_shapes=[pltpu.VMEM((128, border.shape[1]), BF)],
        input_output_aliases={4: 0},
        compiler_params=pltpu.CompilerParams(vmem_limit_bytes=32 << 20),
        name="finish",
    )(border, last, window, strength, volume)


def reduce_kernel(dims, in_ref, out_ref, near_ref, far_ref, mid_ref, send1, recv1, send2, recv2):
    ny, nz, nx, ng = dims
    plane = ny * nx * ng
    place, core = lax.axis_index("space"), lax.axis_index("grp")
    y, z, x = place // (nz * nx), (place // nx) % nz, place % nx
    me = (y * nx + x) * ng + core

    hop = lambda step, size: min(step, size - step)
    steps = sorted(((dy, dx, dg) for dy in range(ny) for dx in range(nx) for dg in range(ng)),
                   key=lambda d: -hop(d[0], ny) - hop(d[1], nx))
    steps = [d for d in steps if d != (0, 0, 0)]
    ys = [(y + d) % ny for d in range(ny)]
    xs = [(x + d) % nx for d in range(nx)]
    gs = [(core + d) % ng for d in range(ng)]
    zs = [(z + d) % nz for d in range(nz)]
    near = [((ys[dy] * nz + z) * nx + xs[dx], gs[dg]) for dy, dx, dg in steps]
    slots = [(ys[dy] * nx + xs[dx]) * ng + gs[dg] for dy, dx, dg in steps]
    reach = sorted(range(1, nz), key=lambda d: -hop(d, nz))
    far = [((y * nz + zs[d]) * nx + x, core) for d in reach]

    barrier = pltpu.get_barrier_semaphore()
    for peer in far + near:
        pl.semaphore_signal(barrier, inc=1, device_id=peer, device_id_type=pl.DeviceIdType.MESH)
    near_ref[me] = in_ref[0]
    pl.semaphore_wait(barrier, len(near) + len(far))

    def near_copy(j, slot):
        return pltpu.make_async_remote_copy(
            src_ref=in_ref.at[0], dst_ref=near_ref.at[slot], send_sem=send1.at[j], recv_sem=recv1.at[slot],
            device_id=near[j], device_id_type=pl.DeviceIdType.MESH)

    def far_copy(j, slot):
        return pltpu.make_async_remote_copy(
            src_ref=mid_ref.at[0], dst_ref=far_ref.at[slot], send_sem=send2.at[j], recv_sem=recv2.at[slot],
            device_id=far[j], device_id_type=pl.DeviceIdType.MESH)

    for j in range(len(near)):
        near_copy(j, me).start()
    for j in range(len(near)):
        near_copy(j, slots[j]).wait_recv()
    part = jnp.sum(near_ref[...], axis=0)
    mid_ref[0] = part
    far_ref[z] = part
    for j in range(len(far)):
        far_copy(j, z).start()
    for j in range(len(near)):
        near_copy(j, me).wait_send()
    for j in range(len(far)):
        far_copy(j, zs[reach[j]]).wait_recv()
    total = jnp.sum(jnp.sum(far_ref[...], axis=0), axis=1, keepdims=True)
    out_ref[...] = jnp.broadcast_to(total, out_ref.shape)
    for j in range(len(far)):
        far_copy(j, z).wait_send()


def total_of(parts, dims):
    ny, nz, nx, ng = dims
    plane = ny * nx * ng
    vm = pl.BlockSpec(memory_space=pltpu.VMEM)
    return pl.pallas_call(
        functools.partial(reduce_kernel, dims),
        in_specs=[vm],
        out_specs=vm,
        out_shape=jax.ShapeDtypeStruct((1, 128), F32),
        scratch_shapes=[pltpu.VMEM((plane, 1, 128), F32), pltpu.VMEM((nz, 1, 128), F32), pltpu.VMEM((1, 1, 128), F32),
                        pltpu.SemaphoreType.DMA((plane,)), pltpu.SemaphoreType.DMA((plane,)),
                        pltpu.SemaphoreType.DMA((nz,)), pltpu.SemaphoreType.DMA((nz,))],
        compiler_params=pltpu.CompilerParams(collective_id=0, has_side_effects=True),
        name="total",
    )(parts)


def shards(dims, echoes, frame_count, clutter_rank, noise_rank, start_basis):
    n, frames, width = echoes.shape
    half = width // 2
    devices = dims[0] * dims[1] * dims[2] * dims[3]
    spot = np.arange(width, dtype=np.float64)
    window = jnp.asarray((np.sin(np.pi * (spot + 0.5) / width) ** 2).astype(np.float32)[None])

    def slot_of(b):
        return (lax.axis_index("space") * dims[3] + lax.axis_index("grp")) * n + b

    far = lambda a: pltpu.with_memory_space_constraint(a, pltpu.HBM)
    st, s, border, masked = subspace(far(echoes), far(frame_count), far(clutter_rank), far(noise_rank),
                                     far(start_basis.T), slot_of)
    back = [(d + 1, d) for d in range(devices - 1)]
    border = lax.ppermute(border, ("space", "grp"), back)
    volume, strength, last = project(masked, frames, st, s, clutter_rank, noise_rank, window, slot_of)
    volume, strength, parts = finish(border, last, window, strength, volume, n)
    total = total_of(parts, dims)[0, 0]
    power = strength.reshape(-1) / (total / (devices * n * half) + 1e-6)
    return volume, power


def solution(mesh):
    dims = (4, 8, 4, mesh.shape["grp"])
    both = ("space", "grp")
    return jax.shard_map(
        functools.partial(shards, dims), mesh=mesh,
        in_specs=(P(both, None, None), P(), P(), P(), P()),
        out_specs=(P(None, both), P(both)), check_vma=False)
```

time: 76.1 us -> 64.8 us (0.85)
  Pallas kernels: 66.1 us -> 56.9 us
  local copies, waits for them, and re-layouts: 2.53 us -> 0.52 us
    pallas_call x2, Pallas kernels: 45.5 us -> 36.9 us  [the longest x1 29.5 us: subspace(): pl.pallas_call(functools.partial(subspace_kernel, n, count_of), grid=(n,)...]
    unnamed x8, local copies, waits for them, and re-layouts: 2.53 us -> 0.52 us
  transfers between devices with their start and end apart: 1 -> 1, of which waited for: 0 -> 0; matrix products, arithmetic and copies ran while one was open for 0% -> 0% of each run, Pallas kernels for 13% -> 11%
where the time goes in v3:
time: 64.8 us; the launch traced here: 64.6 us
  Pallas kernels  56.9 us (88%)
  starting transfers between devices  5.29 us (8%)
  between operations  1.27 us (2%)
    pallas_call x1, Pallas kernels, subspace(): pl.pallas_call(functools.partial(subspace_kernel, n, count_of), grid=(n,)...  29.5 us
    pallas_call x1, Pallas kernels, total_of(): pl.pallas_call(functools.partial(reduce_kernel, dims), in_specs=[vm], out...  18.5 us
    pallas_call x1, Pallas kernels, project(): pl.pallas_call(functools.partial(project_kernel, n, frames, count_of), gr...  7.37 us
    ppermute x1, starting transfers between devices, shards(): border = lax.ppermute(border, ('space', 'grp'), back)  5.29 us
    pallas_call x1, Pallas kernels, finish(): pl.pallas_call(functools.partial(border_kernel, n), grid=(1,), in_specs=[...  1.51 us
  transfers between devices with their start and end apart: 1, of which 0 were waited for; matrix products, arithmetic and copies ran while one was open for 0% of the time, Pallas kernels for 11%

profile of v3, /device:TPU:1, one launch (start us, length us, event | category | flops | bytes accessed | tf_op | source)
XLA Modules:
  0.0 64.6 jit_solution(4381542278211886310)
XLA Ops:
  0.6 0.0 copy-start.2
  0.6 0.0 copy-start.1
  0.7 0.0 copy-start
  0.7 29.5 %subspace.1 = (bf16[5,128,384]{2,1,0:T(8,128)(2,1)S(1)}, bf16[5,384,128]{2,1,0:T(8,128)(2,1)S(1)}, bf16[96,1408]{1,0:T(8,128)(2,1)S(1)}, bf16[5,384,2048]{2,1,0:T(8,128)(2,1)S(1)}) custom-call(bf16[5,300,2048]{2,1,0:T(8,128)(2,1)} %echo_ref.1, s32[1280]{0:T(1024)} %refs_0_.1, s32[1280]{0:T(1024)} %cr_ref.1, s32[1280]{0:T(1024)} %nr_ref.1, f32[96,300]{1,0:T(8,128)} %bitcast.4), custom_call_target="tpu_custom_call" | custom-call | tf_op jit(solution)/shard_map/subspace/pallas_call | solution.py:267
  30.2 5.3 %collective-permute-start = (bf16[96,1408]{1,0:T(8,128)(2,1)S(1)}, bf16[96,1408]{1,0:T(8,128)(2,1)S(1)}, u32[]{:S(2)}, u32[]{:S(2)}) collective-permute-start(bf16[96,1408]{1,0:T(8,128)(2,1)S(1)} %get-tuple-element.12), channel_id=1, source_target_pairs={{1,0},{2,1},{3,2},{4,3},{5,4},{6,5},{7,6},{8,7},{9,8},{10,9},{11,1... | collective-permute-start | bytes 811016 | tf_op jit(solution)/shard_map/ppermute | solution.py:486
  35.5 0.0 copy-done.2
  35.5 0.0 copy-done.1
  35.5 0.0 copy-done
  35.5 7.4 %project.1 = (f32[300,5120]{1,0:T(8,128)}, f32[1,5120]{1,0:T(1,128)S(1)}, f32[304,1024]{1,0:T(8,128)S(1)}) custom-call(bf16[5,384,2048]{2,1,0:T(8,128)(2,1)S(1)} %get-tuple-element.13.x_ref, bf16[5,128,384]{2,1,0:T(8,128)(2,1)S(1)} %get-tuple-element.14.st_ref, bf16[5,384,128]{2,1,0:T(8,128)(2,1)S(1)} %get-tuple-element.15.s_ref, s32[1280]{0:T(1024)S(1)} %copy-done, ...), custom_call_target="tpu_custom_call" | custom-call | flops 8000000000 | bytes 12000000 | tf_op jit(solution)/shard_map/project/pallas_call | solution.py:335
  42.9 0.0 collective-permute-done.border_ref
  42.9 1.5 %finish.1 = (f32[300,5120]{1,0:T(8,128)}, f32[1,5120]{1,0:T(1,128)S(1)}, f32[1,1,128]{2,1,0:T(1,128)S(1)}) custom-call(bf16[96,1408]{1,0:T(8,128)(2,1)S(1)} %collective-permute-done.border_ref, f32[304,1024]{1,0:T(8,128)S(1)} %get-tuple-element.16.last_ref, f32[1,2048]{1,0:T(1,128)S(1)} %copy-done.2, ...), custom_call_target="tpu_custom_call", output_to_operand_aliasing={{0}: (4, {})} | custom-call | tf_op jit(solution)/shard_map/finish/pallas_call | solution.py:385
  44.4 0.0 copy-start.3
  44.4 0.5 copy-done.3
  44.9 18.5 %total.1 = f32[1,128]{1,0:T(1,128)} custom-call(f32[1,1,128]{2,1,0:T(1,128)} %copy-done.3), custom_call_target="tpu_custom_call" | custom-call | tf_op jit(solution)/shard_map/total/pallas_call | solution.py:459
  64.0 0.6 broadcast_divide_fusion
Async XLA Ops:
  0.6 34.8 %copy-start.2 = (f32[1,2048]{1,0:T(1,128)S(1)}, f32[1,2048]{1,0:T(1,128)}, u32[]{:S(2)}) copy-start(f32[1,2048]{1,0:T(1,128)} %constant.9.clone.win_ref) | copy-start | bytes 24580
  0.6 34.8 %copy-start.1 = (s32[1280]{0:T(1024)S(1)}, s32[1280]{0:T(1024)}, u32[]{:S(2)}) copy-start(s32[1280]{0:T(1024)} %nr_ref.1) | copy-start | bytes 15364
  0.7 34.8 %copy-start = (s32[1280]{0:T(1024)S(1)}, s32[1280]{0:T(1024)}, u32[]{:S(2)}) copy-start(s32[1280]{0:T(1024)} %cr_ref.1) | copy-start | bytes 15364
  30.2 12.7 %collective-permute-start = (bf16[96,1408]{1,0:T(8,128)(2,1)S(1)}, bf16[96,1408]{1,0:T(8,128)(2,1)S(1)}, u32[]{:S(2)}, u32[]{:S(2)}) collective-permute-start(bf16[96,1408]{1,0:T(8,128)(2,1)S(1)} %get-tuple-element.12), channel_id=1, source_target_pairs={{1,0},{2,1},{3,2},{4,3},{5,4},{6,5},{7,6},{8,7},{9,8},{10,9},{11,1... | collective-permute-start | bytes 811016 | tf_op jit(solution)/shard_map/ppermute | solution.py:486
  44.4 0.5 copy-start.3

commit v4 on v3

--- a/solution.py
+++ b/solution.py
@@ -39,15 +39,14 @@
     sub = lax.broadcasted_iota(jnp.int32, (8, 128), 0)
     place = lax.broadcasted_iota(jnp.int32, (8, 128), 1)
     lane = place & (GAP - 1)
+    tile = {(b, t): m_ref[b, 8 * t:8 * t + 8, :] for b in pairs for t in range(tiles)}
     for p in range(tiles):
         j0 = 8 * p
         inside = (lane >= j0) & (lane < j0 + 8)
         eye = jnp.where(lane == j0 + sub, 1.0, 0.0)
         between(p)
-        cols, diag, tile, inverses, pivots = {}, {}, {}, {}, {}
+        cols, diag, inverses, pivots, ahead = {}, {}, {}, {}, {}
         for b in pairs:
-            for t in range(p, tiles):
-                tile[b, t] = m_ref[b, 8 * t:8 * t + 8, :]
             diag[b] = jnp.where(inside, eye, tile[b, p])
         for q in range(8):
             pick = place - lane + (j0 + q)
@@ -56,12 +55,15 @@
                     cols[b, q, t] = jnp.take_along_axis(tile[b, t], pick, axis=1)
         for q in range(8):
             for b in pairs:
-                pivot = spread(cols[b, q, p], q)
+                pivot = spread(cols[b, 0, p], 0) if q == 0 else ahead[b]
                 inv = 1.0 / pivot
                 pivots[b] = pivot if q == 0 else jnp.where(sub == q, pivot, pivots[b])
                 inverses[b] = inv if q == 0 else jnp.where(sub == q, inv, inverses[b])
                 if q < 7:
-                    f = jnp.where(sub > q, cols[b, q, p] * inv, 0.0)
+                    nxt = cols[b, q + 1, p]
+                    cross = spread(cols[b, q, p], q + 1) * spread(nxt, q)
+                    ahead[b] = spread(nxt, q + 1) - cross * inv
+                    f = jnp.where(sub > q, cols[b, q, p], 0.0) * inv
                     for q2 in range(q + 1, 8):
                         cols[b, q2, p] = cols[b, q2, p] - f * spread(cols[b, q2, p], q)
                     diag[b] = diag[b] - f * spread(diag[b], q)
@@ -72,15 +74,15 @@
             break
         for b in pairs:
             solved = diag[b] * inverses[b]
-            for q in range(7, 0, -1):
-                g = jnp.where(sub < q, cols[b, q, p] * inverses[b], 0.0)
-                solved = solved - g * spread(solved, q)
-            rows = [spread(solved, q) for q in range(8)]
-            for t in range(p + 1, tiles):
-                rest = jnp.where(inside, 0.0, tile[b, t])
-                for q in range(8):
-                    rest = rest - cols[b, q, t] * rows[q]
-                m_ref[b, 8 * t:8 * t + 8, :] = rest
+            rest = {t: jnp.where(inside, 0.0, tile[b, t]) for t in range(p + 1, tiles)}
+            for q in range(7, -1, -1):
+                row = spread(solved, q)
+                if q:
+                    solved = solved - jnp.where(sub < q, cols[b, q, p] * inverses[b], 0.0) * row
+                for t in rest:
+                    rest[t] = rest[t] - cols[b, q, t] * row
+            for t in rest:
+                tile[b, t] = rest[t]
 
 
 def mm3(a, b, dims=NN):
@@ -93,9 +95,10 @@
 def mm6(a, b, dims=NN):
     (ah, am, al), (bh, bm, bl) = a, b
     m = ah.shape[0]
-    first = mm(jnp.concatenate([ah, am, al], axis=0), bh, dims)
-    second = mm(jnp.concatenate([ah, am], axis=0), bm, dims)
-    return first[:m] + (first[m:2 * m] + second[:m]) + (second[m:] + first[2 * m:] + mm(ah, bl, dims))
+    pair = jnp.concatenate([bh, bm], axis=0 if dims is NT else 1)
+    first = mm(jnp.concatenate([ah, am, al], axis=0), pair, dims)
+    high, mid = first[:, :128], first[:, 128:]
+    return high[:m] + (high[m:2 * m] + mid[:m]) + (mid[m:2 * m] + high[2 * m:] + mm(ah, bl, dims))
 
 
 def both(parts, h):
@@ -162,11 +165,11 @@
 
         y_ref[0, 0, :, :] = jnp.zeros((128, lp), F32)
         y_ref[0, 0, :k, :frames] = start_ref[...]
-        start = split(y_ref[0, 0])
+        start = split(y_ref[0, 0, :k, :])
         y_ref[...] = jnp.zeros_like(y_ref)
         p_ref[...] = jnp.zeros_like(p_ref)
         for b in range(n):
-            place(p_ref, b, mm3(start, (gh_ref[b], gl_ref[b]))[:k])
+            place(p_ref, b, mm3(start, (gh_ref[b], gl_ref[b])))
 
         def forward(b):
             i, at = spots[b][0]
@@ -295,6 +298,7 @@
     @pl.when(step == 0)
     def _():
         coef_ref[...] = jnp.zeros_like(coef_ref)
+        prev_ref[...] = jnp.zeros_like(prev_ref)
 
     slot = count_of(step)
     band = band_of(k, cr_ref[slot], nr_ref[slot])
@@ -303,18 +307,14 @@
         at = slice(c * CHUNK, (c + 1) * CHUNK)
         coef_ref[:k, at] = (mm(st, x_ref[0, :, at], NN) * band).astype(BF)
 
-    @pl.when(step > 0)
-    def _():
-        for c in range(half // CHUNK):
-            at = slice(c * CHUNK, (c + 1) * CHUNK)
-            low = mm(s, coef_ref[:, at], NN).astype(BF).astype(F32)
-            vol = (prev_ref[:, at] + low * win_ref[:, at])[:frames]
-            vol_ref[:, at] = vol
-            str_ref[:, at] = jnp.sum(vol * vol, axis=0, keepdims=True) / frames
-
     for c in range(half // CHUNK):
         at, up = slice(c * CHUNK, (c + 1) * CHUNK), slice(half + c * CHUNK, half + (c + 1) * CHUNK)
-        prev_ref[:, at] = mm(s, coef_ref[:, up], NN).astype(BF).astype(F32) * win_ref[:, up]
+        low = mm(s, coef_ref[:, at], NN).astype(BF).astype(F32)
+        high = mm(s, coef_ref[:, up], NN).astype(BF).astype(F32)
+        vol = (prev_ref[:, at] + low * win_ref[:, at])[:frames]
+        vol_ref[:, at] = vol
+        str_ref[:, at] = jnp.sum(vol * vol, axis=0, keepdims=True) / frames
+        prev_ref[:, at] = high * win_ref[:, up]
 
     @pl.when(step == n - 1)
     def _():

time: 64.8 us -> 62.5 us (0.965)
  Pallas kernels: 56.9 us -> 54.8 us
    pallas_call x1, Pallas kernels: 29.5 us -> 28 us  [subspace(): pl.pallas_call(functools.partial(subspace_kernel, n, count_of), grid=(n,)...]
    pallas_call x1, Pallas kernels: 7.37 us -> 6.25 us  [project(): pl.pallas_call(functools.partial(project_kernel, n, frames, count_of), gr...]
  transfers between devices with their start and end apart: 1 -> 1, of which waited for: 0 -> 0; matrix products, arithmetic and copies ran while one was open for 0% -> 0% of each run, Pallas kernels for 11% -> 10%
where the time goes in v4:
time: 62.5 us; the launch traced here: 62.3 us
  Pallas kernels  54.8 us (88%)
  starting transfers between devices  5.12 us (8%)
  between operations  1.26 us (2%)
    pallas_call x1, Pallas kernels, subspace(): pl.pallas_call(functools.partial(subspace_kernel, n, count_of), grid=(n,)...  28 us
    pallas_call x1, Pallas kernels, total_of(): pl.pallas_call(functools.partial(reduce_kernel, dims), in_specs=[vm], out...  19.1 us
    pallas_call x1, Pallas kernels, project(): pl.pallas_call(functools.partial(project_kernel, n, frames, count_of), gr...  6.25 us
    ppermute x1, starting transfers between devices, shards(): border = lax.ppermute(border, ('space', 'grp'), back)  5.12 us
    pallas_call x1, Pallas kernels, finish(): pl.pallas_call(functools.partial(border_kernel, n), grid=(1,), in_specs=[...  1.51 us
  transfers between devices with their start and end apart: 1, of which 0 were waited for; matrix products, arithmetic and copies ran while one was open for 0% of the time, Pallas kernels for 10%

profile of v4, /device:TPU:1, one launch (start us, length us, event | category | flops | bytes accessed | tf_op | source)
XLA Modules:
  0.0 62.3 jit_solution(15690279632549014828)
XLA Ops:
  0.6 0.0 copy-start.2
  0.6 0.0 copy-start.1
  0.7 0.0 copy-start
  0.7 28.0 %subspace.1 = (bf16[5,128,384]{2,1,0:T(8,128)(2,1)S(1)}, bf16[5,384,128]{2,1,0:T(8,128)(2,1)S(1)}, bf16[96,1408]{1,0:T(8,128)(2,1)S(1)}, bf16[5,384,2048]{2,1,0:T(8,128)(2,1)S(1)}) custom-call(bf16[5,300,2048]{2,1,0:T(8,128)(2,1)} %echo_ref.1, s32[1280]{0:T(1024)} %refs_0_.1, s32[1280]{0:T(1024)} %cr_ref.1, s32[1280]{0:T(1024)} %nr_ref.1, f32[96,300]{1,0:T(8,128)} %bitcast.4), custom_call_target="tpu_custom_call" | custom-call | tf_op jit(solution)/shard_map/subspace/pallas_call | solution.py:270
  28.6 5.1 %collective-permute-start = (bf16[96,1408]{1,0:T(8,128)(2,1)S(1)}, bf16[96,1408]{1,0:T(8,128)(2,1)S(1)}, u32[]{:S(2)}, u32[]{:S(2)}) collective-permute-start(bf16[96,1408]{1,0:T(8,128)(2,1)S(1)} %get-tuple-element.12), channel_id=1, source_target_pairs={{1,0},{2,1},{3,2},{4,3},{5,4},{6,5},{7,6},{8,7},{9,8},{10,9},{11,1... | collective-permute-start | bytes 811016 | tf_op jit(solution)/shard_map/ppermute | solution.py:486
  33.8 0.0 copy-done.2
  33.8 0.0 copy-done.1
  33.8 0.0 copy-done
  33.8 6.2 %project.1 = (f32[300,5120]{1,0:T(8,128)}, f32[1,5120]{1,0:T(1,128)S(1)}, f32[304,1024]{1,0:T(8,128)S(1)}) custom-call(bf16[5,384,2048]{2,1,0:T(8,128)(2,1)S(1)} %get-tuple-element.13.x_ref, bf16[5,128,384]{2,1,0:T(8,128)(2,1)S(1)} %get-tuple-element.14.st_ref, bf16[5,384,128]{2,1,0:T(8,128)(2,1)S(1)} %get-tuple-element.15.s_ref, s32[1280]{0:T(1024)S(1)} %copy-done, ...), custom_call_target="tpu_custom_call" | custom-call | flops 8000000000 | bytes 12000000 | tf_op jit(solution)/shard_map/project/pallas_call | solution.py:335
  40.0 0.0 collective-permute-done.border_ref
  40.0 1.5 %finish.1 = (f32[300,5120]{1,0:T(8,128)}, f32[1,5120]{1,0:T(1,128)S(1)}, f32[1,1,128]{2,1,0:T(1,128)S(1)}) custom-call(bf16[96,1408]{1,0:T(8,128)(2,1)S(1)} %collective-permute-done.border_ref, f32[304,1024]{1,0:T(8,128)S(1)} %get-tuple-element.16.last_ref, f32[1,2048]{1,0:T(1,128)S(1)} %copy-done.2, ...), custom_call_target="tpu_custom_call", output_to_operand_aliasing={{0}: (4, {})} | custom-call | tf_op jit(solution)/shard_map/finish/pallas_call | solution.py:385
  41.6 0.0 copy-start.3
  41.6 0.5 copy-done.3
  42.1 19.1 %total.1 = f32[1,128]{1,0:T(1,128)} custom-call(f32[1,1,128]{2,1,0:T(1,128)} %copy-done.3), custom_call_target="tpu_custom_call" | custom-call | tf_op jit(solution)/shard_map/total/pallas_call | solution.py:459
  61.7 0.6 %broadcast_divide_fusion = f32[1,5120]{1,0:T(1,128)} fusion(f32[1,5120]{1,0:T(1,128)S(1)} %get-tuple-element.20, f32[]{:T(128)} %bitcast.1), kind=kLoop, calls=%fused_computation | loop fusion | flops 5120 | bytes 40964 | tf_op jit(solution)/shard_map/div | solution.py:490
Async XLA Ops:
  0.6 33.1 %copy-start.2 = (f32[1,2048]{1,0:T(1,128)S(1)}, f32[1,2048]{1,0:T(1,128)}, u32[]{:S(2)}) copy-start(f32[1,2048]{1,0:T(1,128)} %constant.9.clone.win_ref) | copy-start | bytes 24580
  0.6 33.1 %copy-start.1 = (s32[1280]{0:T(1024)S(1)}, s32[1280]{0:T(1024)}, u32[]{:S(2)}) copy-start(s32[1280]{0:T(1024)} %nr_ref.1) | copy-start | bytes 15364
  0.7 33.1 %copy-start = (s32[1280]{0:T(1024)S(1)}, s32[1280]{0:T(1024)}, u32[]{:S(2)}) copy-start(s32[1280]{0:T(1024)} %cr_ref.1) | copy-start | bytes 15364
  28.6 11.4 %collective-permute-start = (bf16[96,1408]{1,0:T(8,128)(2,1)S(1)}, bf16[96,1408]{1,0:T(8,128)(2,1)S(1)}, u32[]{:S(2)}, u32[]{:S(2)}) collective-permute-start(bf16[96,1408]{1,0:T(8,128)(2,1)S(1)} %get-tuple-element.12), channel_id=1, source_target_pairs={{1,0},{2,1},{3,2},{4,3},{5,4},{6,5},{7,6},{8,7},{9,8},{10,9},{11,1... | collective-permute-start | bytes 811016 | tf_op jit(solution)/shard_map/ppermute | solution.py:486
  41.6 0.5 copy-start.3

commit v5 on v4

--- a/solution.py
+++ b/solution.py
@@ -464,7 +464,7 @@
         scratch_shapes=[pltpu.VMEM((plane, 1, 128), F32), pltpu.VMEM((nz, 1, 128), F32), pltpu.VMEM((1, 1, 128), F32),
                         pltpu.SemaphoreType.DMA((plane,)), pltpu.SemaphoreType.DMA((plane,)),
                         pltpu.SemaphoreType.DMA((nz,)), pltpu.SemaphoreType.DMA((nz,))],
-        compiler_params=pltpu.CompilerParams(collective_id=0, has_side_effects=True),
+        compiler_params=pltpu.CompilerParams(collective_id=0, has_side_effects=True, vmem_limit_bytes=8 << 20),
         name="total",
     )(parts)
 

time: 62.5 us -> 60.3 us (0.965)
  Pallas kernels: 54.8 us -> 53.7 us
    pallas_call x1, Pallas kernels: 19.1 us -> 17.9 us  [total_of(): pl.pallas_call(functools.partial(reduce_kernel, dims), in_specs=[vm], out...]
where the time goes in v5:
time: 60.3 us; the launch traced here: 60.1 us
  Pallas kernels  53.7 us (89%)
  starting transfers between devices  5.1 us (8%)
  between operations  0.74 us (1%)
  other arithmetic  0.62 us (1%)
    pallas_call x1, Pallas kernels, subspace(): pl.pallas_call(functools.partial(subspace_kernel, n, count_of), grid=(n,)...  28 us
    pallas_call x1, Pallas kernels, total_of(): pl.pallas_call(functools.partial(reduce_kernel, dims), in_specs=[vm], out...  17.9 us
    pallas_call x1, Pallas kernels, project(): pl.pallas_call(functools.partial(project_kernel, n, frames, count_of), gr...  6.25 us
    ppermute x1, starting transfers between devices, shards(): border = lax.ppermute(border, ('space', 'grp'), back)  5.1 us
    pallas_call x1, Pallas kernels, finish(): pl.pallas_call(functools.partial(border_kernel, n), grid=(1,), in_specs=[...  1.51 us
  transfers between devices with their start and end apart: 1, of which 0 were waited for; matrix products, arithmetic and copies ran while one was open for 0% of the time, Pallas kernels for 10%

profile of v5, /device:TPU:1, one launch (start us, length us, event | category | flops | bytes accessed | tf_op | source)
XLA Modules:
  0.0 60.1 jit_solution(15626883948976124407)
XLA Ops:
  0.6 0.0 copy-start.2
  0.6 0.0 copy-start.1
  0.7 0.0 copy-start
  0.7 28.0 %subspace.1 = (bf16[5,128,384]{2,1,0:T(8,128)(2,1)S(1)}, bf16[5,384,128]{2,1,0:T(8,128)(2,1)S(1)}, bf16[96,1408]{1,0:T(8,128)(2,1)S(1)}, bf16[5,384,2048]{2,1,0:T(8,128)(2,1)S(1)}) custom-call(bf16[5,300,2048]{2,1,0:T(8,128)(2,1)} %echo_ref.1, s32[1280]{0:T(1024)} %refs_0_.1, s32[1280]{0:T(1024)} %cr_ref.1, s32[1280]{0:T(1024)} %nr_ref.1, f32[96,300]{1,0:T(8,128)} %bitcast.5), custom_call_target="tpu_custom_call" | custom-call | tf_op jit(solution)/shard_map/subspace/pallas_call | solution.py:270
  28.7 5.1 %collective-permute-start = (bf16[96,1408]{1,0:T(8,128)(2,1)S(1)}, bf16[96,1408]{1,0:T(8,128)(2,1)S(1)}, u32[]{:S(2)}, u32[]{:S(2)}) collective-permute-start(bf16[96,1408]{1,0:T(8,128)(2,1)S(1)} %get-tuple-element.12), channel_id=1, source_target_pairs={{1,0},{2,1},{3,2},{4,3},{5,4},{6,5},{7,6},{8,7},{9,8},{10,9},{11,1... | collective-permute-start | bytes 811016 | tf_op jit(solution)/shard_map/ppermute | solution.py:486
  33.8 0.0 copy-done.2
  33.8 0.0 copy-done.1
  33.8 0.0 copy-done
  33.8 6.2 %project.1 = (f32[300,5120]{1,0:T(8,128)}, f32[1,5120]{1,0:T(1,128)S(1)}, f32[304,1024]{1,0:T(8,128)S(1)}) custom-call(bf16[5,384,2048]{2,1,0:T(8,128)(2,1)S(1)} %get-tuple-element.13.x_ref, bf16[5,128,384]{2,1,0:T(8,128)(2,1)S(1)} %get-tuple-element.14.st_ref, bf16[5,384,128]{2,1,0:T(8,128)(2,1)S(1)} %get-tuple-element.15.s_ref, s32[1280]{0:T(1024)S(1)} %copy-done, ...), custom_call_target="tpu_custom_call" | custom-call | flops 8000000000 | bytes 12000000 | tf_op jit(solution)/shard_map/project/pallas_call | solution.py:335
  40.0 0.0 collective-permute-done.border_ref
  40.0 1.5 %finish.1 = (f32[300,5120]{1,0:T(8,128)}, f32[1,5120]{1,0:T(1,128)S(1)}, f32[1,1,128]{2,1,0:T(1,128)S(1)}) custom-call(bf16[96,1408]{1,0:T(8,128)(2,1)S(1)} %collective-permute-done.border_ref, f32[304,1024]{1,0:T(8,128)S(1)} %get-tuple-element.16.last_ref, f32[1,2048]{1,0:T(1,128)S(1)} %copy-done.2, ...), custom_call_target="tpu_custom_call", output_to_operand_aliasing={{0}: (4, {})} | custom-call | tf_op jit(solution)/shard_map/finish/pallas_call | solution.py:385
  41.5 17.9 %total.1 = f32[1,128]{1,0:T(1,128)S(1)} custom-call(f32[1,1,128]{2,1,0:T(1,128)S(1)} %get-tuple-element.21.in_ref), custom_call_target="tpu_custom_call" | custom-call | tf_op jit(solution)/shard_map/total/pallas_call | solution.py:459
  59.5 0.6 %broadcast_divide_fusion = f32[1,5120]{1,0:T(1,128)} fusion(f32[1,5120]{1,0:T(1,128)S(1)} %get-tuple-element.20, f32[]{:T(128)} %bitcast.1), kind=kLoop, calls=%fused_computation | loop fusion | flops 5120 | bytes 40964 | tf_op jit(solution)/shard_map/div | solution.py:490
Async XLA Ops:
  0.6 33.1 %copy-start.2 = (f32[1,2048]{1,0:T(1,128)S(1)}, f32[1,2048]{1,0:T(1,128)}, u32[]{:S(2)}) copy-start(f32[1,2048]{1,0:T(1,128)} %constant.9.clone.win_ref) | copy-start | bytes 24580
  0.6 33.1 %copy-start.1 = (s32[1280]{0:T(1024)S(1)}, s32[1280]{0:T(1024)}, u32[]{:S(2)}) copy-start(s32[1280]{0:T(1024)} %nr_ref.1) | copy-start | bytes 15364
  0.7 33.1 %copy-start = (s32[1280]{0:T(1024)S(1)}, s32[1280]{0:T(1024)}, u32[]{:S(2)}) copy-start(s32[1280]{0:T(1024)} %cr_ref.1) | copy-start | bytes 15364
  28.7 11.4 %collective-permute-start = (bf16[96,1408]{1,0:T(8,128)(2,1)S(1)}, bf16[96,1408]{1,0:T(8,128)(2,1)S(1)}, u32[]{:S(2)}, u32[]{:S(2)}) collective-permute-start(bf16[96,1408]{1,0:T(8,128)(2,1)S(1)} %get-tuple-element.12), channel_id=1, source_target_pairs={{1,0},{2,1},{3,2},{4,3},{5,4},{6,5},{7,6},{8,7},{9,8},{10,9},{11,1... | collective-permute-start | bytes 811016 | tf_op jit(solution)/shard_map/ppermute | solution.py:486
